TPU v7x, 32 devices: a whole 2x2x4 slice. The times are simulated.
32 devices in a mesh: dp: 16 (over z, x, core), tensor: 2 (over y).
Axes of the slice: x: 2, y: 2, z: 4, core: 2. Of those that a mesh axis runs over, the one named last changes fastest.
Arguments:
- features: bfloat16 [32, 256, 512], P('dp'), may hold values from -6 to 6
- mask_starts: int32 [32, 16], P('dp'), may hold values from 0 to 246, as said below
- block_slot: int32 [50], replicated, may hold values from 0 to 63, as said below
- settings: float32 [2], replicated, may hold values from 0.05 to 0.9, as said below
- matrices: float32 [64, 2, 384, 384], P('dp', 'tensor'), may hold values from -0.21875 to 0.21875
- momentum: float32 [64, 2, 384, 384], P('dp', 'tensor'), may hold values from -0.078125 to 0.078125
- statistics: float32 [64, 2, 2, 384, 384], P('dp', 'tensor'), may hold values from -5e-08 to 1.5e-07, as said below
- inverse_roots: float32 [64, 2, 2, 384, 384], P('dp', 'tensor'), may hold values from -13 to 43, as said below
- teacher: float32 [64, 2, 384, 384], P('dp', 'tensor'), may hold values from -0.21875 to 0.21875
- dense_params: float32 [768, 1435], P('dp'), may hold values from -4 to 4
- dense_moment: float32 [768, 1435], P('dp'), may hold values from -0.00030517578 to 0.00030517578
- dense_second: float32 [768, 1435], P('dp'), may hold values from 1e-11 to 1e-09
- teacher_dense: float32 [768, 1435], P('dp'), may hold values from -4 to 4
Outputs:
- loss_value: float32 [], replicated
- grad_norm: float32 [], replicated
- matrices_new: float32 [64, 2, 384, 384], P('dp', 'tensor')
- momentum_new: float32 [64, 2, 384, 384], P('dp', 'tensor')
- statistics_new: float32 [64, 2, 2, 384, 384], P('dp', 'tensor')
- teacher_new: float32 [64, 2, 384, 384], P('dp', 'tensor')
- dense_new: float32 [768, 1435], P('dp')
- dense_moment_new: float32 [768, 1435], P('dp')
- dense_second_new: float32 [768, 1435], P('dp')
- teacher_dense_new: float32 [768, 1435], P('dp')
Inputs may be any that keep to these rules, and one draw needn't show every extreme that they name: `mask_starts`: starts of a clip may repeat. `block_slot`: 50 distinct slot numbers, one a block. `settings`: the teacher's rate first, the clipping threshold second. `statistics`: symmetric. `inverse_roots`: symmetric.
All inputs are finite; a program needn't handle non-finite values.
Results may differ from a plain program's by a relative error of at most 0.012.
Values may be sent and summed in bfloat16 or wider, within the bound.
A program may use at most 384 MiB of HBM per device.

v0:
```python
import math

import jax
import jax.numpy as jnp
from jax import lax
from jax.sharding import PartitionSpec as P

D = 768
HD = 64
FF = 3072
C = 512
KERNEL = 19
GROUPS = 16
LAYERS = 2
MICRO = 2
MASK_LEN = 10
BLK = 384
GW = 48


norm_eps = 1e-05
loss_beta = 0.25
state_decay = 0.5
matrix_rate = 1.0
dense_rate = 0.01
adam_eps = 1e-08


def norm_rows(values, gain_row, shift_row):
    center = values - jnp.mean(values, axis=-1, keepdims=True)
    spread = lax.rsqrt(jnp.mean(center * center, axis=-1, keepdims=True) + norm_eps)
    return center * spread * gain_row + shift_row


def tile_blocks(blocks, row_count, col_count):
    return (
        blocks.reshape(row_count, col_count, BLK, BLK)
        .transpose(0, 2, 1, 3)
        .reshape(row_count * BLK, col_count * BLK)
    )


def untile(matrix, row_count, col_count):
    return (
        matrix.reshape(row_count, BLK, col_count, BLK)
        .transpose(0, 2, 1, 3)
        .reshape(row_count * col_count, BLK, BLK)
    )


def block_counts():
    return (D // BLK, D // (2 * BLK), FF // (2 * BLK))


def unpack_half(blocks):
    row_blocks, col_blocks, ff_blocks = block_counts()
    layers_out = []
    offset = 0
    for layer_idx in range(LAYERS):
        count_qkv = row_blocks * col_blocks
        qkv_weight = jnp.stack(
            [
                tile_blocks(
                    blocks[offset + which_proj * count_qkv : offset + (which_proj + 1) * count_qkv],
                    row_blocks,
                    col_blocks,
                )
                for which_proj in range(3)
            ]
        )
        offset += 3 * count_qkv
        out_weight = tile_blocks(
            blocks[offset : offset + col_blocks * row_blocks], col_blocks, row_blocks
        )
        offset += col_blocks * row_blocks
        in_weight = tile_blocks(
            blocks[offset : offset + row_blocks * ff_blocks], row_blocks, ff_blocks
        )
        offset += row_blocks * ff_blocks
        down_weight = tile_blocks(
            blocks[offset : offset + ff_blocks * row_blocks], ff_blocks, row_blocks
        )
        offset += ff_blocks * row_blocks
        layers_out.append((qkv_weight, out_weight, in_weight, down_weight))
    head_weight = tile_blocks(
        blocks[offset : offset + row_blocks * col_blocks], row_blocks, col_blocks
    )
    return (layers_out, head_weight)


def pack_half(layer_grads, head_grad):
    row_blocks, col_blocks, ff_blocks = block_counts()
    pieces = []
    for qkv_grad, out_grad, in_grad, down_grad in layer_grads:
        for which_proj in range(3):
            pieces.append(untile(qkv_grad[which_proj], row_blocks, col_blocks))
        pieces.append(untile(out_grad, col_blocks, row_blocks))
        pieces.append(untile(in_grad, row_blocks, ff_blocks))
        pieces.append(untile(down_grad, ff_blocks, row_blocks))
    pieces.append(untile(head_grad, row_blocks, col_blocks))
    return jnp.concatenate(pieces, axis=0)


def params_of(slots_low, cols_low, block_slot):
    picked = jnp.take(slots_low[:, 0], block_slot, axis=0)
    layers_half, head_weight = unpack_half(picked)
    conv_end = C + KERNEL * GW
    proj_weight = cols_low[:, :C].T
    conv_weight = cols_low[:, C:conv_end].reshape(GROUPS, GW, KERNEL, GW)
    vectors = cols_low[:, conv_end:].T
    return (layers_half, head_weight, (proj_weight, conv_weight, vectors))


def pad_frames(values):
    margin = KERNEL // 2
    clip_count, frames = (values.shape[0], values.shape[1])
    padded = jnp.pad(values, ((0, 0), (margin, margin), (0, 0)))
    return padded.reshape(clip_count, frames + 2 * margin, GROUPS, GW)


def conv_apply(padded, conv_weight, frames):
    total = jnp.zeros((padded.shape[0], frames, GROUPS, GW), jnp.float32)
    for tap in range(KERNEL):
        total = total + jnp.einsum(
            "bfgi,goi->bfgo",
            padded[:, tap : tap + frames],
            conv_weight[:, :, tap],
            preferred_element_type=jnp.float32,
        )
    return total


def span_mask(mask_starts, frames):
    positions = jnp.arange(frames, dtype=jnp.int32)[None, :, None]
    starts = mask_starts[:, None, :]
    inside = (positions >= starts) & (positions < starts + MASK_LEN)
    return jnp.any(inside, axis=-1).astype(jnp.float32)


def branch_total(partial_value):
    return lax.psum(partial_value.astype(jnp.bfloat16), "tensor").astype(jnp.float32)


def input_total(partial_value):
    return lax.psum(partial_value.astype(jnp.bfloat16), "tensor").astype(jnp.float32)


def teacher_targets(branches, clip_count, frames):
    summed = jnp.zeros((clip_count, frames, D), jnp.float32)
    for branch in branches:
        shaped = branch.reshape(clip_count, frames, D)
        center = shaped - jnp.mean(shaped, axis=1, keepdims=True)
        summed = summed + center * lax.rsqrt(
            jnp.mean(center * center, axis=1, keepdims=True) + norm_eps
        )
    return summed / len(branches)


def forward(params, inputs, mask_micro, keep):
    layers_half, head_weight, (proj_weight, conv_weight, vectors) = params
    vec_rows = vectors.astype(jnp.float32)
    score_scale = 1.0 / math.sqrt(HD)
    clip_count, frames = (inputs.shape[0], inputs.shape[1])
    row_total = clip_count * frames
    projected = jnp.einsum("bfc,cd->bfd", inputs, proj_weight, preferred_element_type=jnp.float32)
    embedded = jnp.where(mask_micro[..., None] > 0, vec_rows[0], projected)
    padded_low = pad_frames(embedded.astype(jnp.bfloat16))
    conv_out = conv_apply(padded_low, conv_weight, frames).reshape(clip_count, frames, D)
    hidden = (embedded + jax.nn.gelu(conv_out)).reshape(row_total, D)
    branches = []
    saved = []
    for layer_idx, (qkv_weight, out_weight, in_weight, down_weight) in enumerate(layers_half):
        gain_at = 1 + 4 * layer_idx
        heads_half = qkv_weight.shape[-1] // HD
        normed_low = norm_rows(hidden, vec_rows[gain_at], vec_rows[gain_at + 1]).astype(
            jnp.bfloat16
        )
        projected_qkv = jnp.einsum(
            "td,wde->wte", normed_low, qkv_weight, preferred_element_type=jnp.float32
        ).astype(jnp.bfloat16)
        shaped = projected_qkv.reshape(3, clip_count, frames, heads_half, HD)
        scores = (
            jnp.einsum("bqhd,bkhd->bhqk", shaped[0], shaped[1], preferred_element_type=jnp.float32)
            * score_scale
        )
        top_log = jax.nn.logsumexp(scores, axis=-1)
        attn_probs = jnp.exp(scores - top_log[..., None])
        mixed_heads = jnp.einsum(
            "bhqk,bkhd->bqhd",
            attn_probs.astype(jnp.bfloat16),
            shaped[2],
            preferred_element_type=jnp.float32,
        )
        mixed_heads = mixed_heads.astype(jnp.bfloat16).reshape(row_total, qkv_weight.shape[-1])
        attention = branch_total(
            jnp.dot(mixed_heads, out_weight, preferred_element_type=jnp.float32)
        )
        residual = hidden + attention
        normed_mlp = norm_rows(residual, vec_rows[gain_at + 2], vec_rows[gain_at + 3]).astype(
            jnp.bfloat16
        )
        hidden_pre = jnp.dot(normed_mlp, in_weight, preferred_element_type=jnp.float32)
        activated = jax.nn.gelu(hidden_pre).astype(jnp.bfloat16)
        branch = branch_total(jnp.dot(activated, down_weight, preferred_element_type=jnp.float32))
        branches.append(branch)
        if keep:
            saved.append(
                (
                    hidden,
                    normed_low,
                    shaped,
                    top_log,
                    mixed_heads,
                    residual,
                    normed_mlp,
                    hidden_pre,
                    activated,
                )
            )
        hidden = residual + branch
    return (hidden, branches, (saved, embedded, padded_low, conv_out))


def student_step(params, inputs, mask_micro, target, loss_scale):
    layers_half, head_weight, (proj_weight, conv_weight, vectors) = params
    vec_rows = vectors.astype(jnp.float32)
    score_scale = 1.0 / math.sqrt(HD)
    clip_count, frames = (inputs.shape[0], inputs.shape[1])
    row_total = clip_count * frames
    hidden, _, (saved, embedded, padded_low, conv_out) = forward(params, inputs, mask_micro, True)
    vec_grads = [None] * vectors.shape[0]
    final_at = 1 + 4 * len(layers_half)
    final_low = norm_rows(hidden, vec_rows[final_at], vec_rows[final_at + 1]).astype(jnp.bfloat16)
    predicted = jnp.dot(final_low, head_weight, preferred_element_type=jnp.float32)
    half_width = head_weight.shape[1]
    target_half = lax.dynamic_slice_in_dim(
        target, lax.axis_index("tensor") * half_width, half_width, axis=1
    )
    mismatch = predicted - target_half
    magnitude = jnp.abs(mismatch)
    row_mask = mask_micro.reshape(row_total, 1)
    penalty = jnp.where(
        magnitude < loss_beta, 0.5 * mismatch * mismatch / loss_beta, magnitude - 0.5 * loss_beta
    )
    loss_add = jnp.sum(penalty * row_mask) * loss_scale
    grad_predicted = (row_mask * jnp.clip(mismatch / loss_beta, -1.0, 1.0) * loss_scale).astype(
        jnp.bfloat16
    )
    head_grad = jnp.einsum(
        "td,te->de", final_low, grad_predicted, preferred_element_type=jnp.float32
    )
    grad_final = input_total(
        jnp.einsum("te,de->td", grad_predicted, head_weight, preferred_element_type=jnp.float32)
    )
    _, pullback = jax.vjp(norm_rows, hidden, vec_rows[final_at], vec_rows[final_at + 1])
    grad_hidden, vec_grads[final_at], vec_grads[final_at + 1] = pullback(grad_final)
    layer_grads = []
    for layer_idx in reversed(range(len(layers_half))):
        qkv_weight, out_weight, in_weight, down_weight = layers_half[layer_idx]
        (
            hidden_in,
            normed_low,
            shaped,
            top_log,
            mixed_heads,
            residual,
            normed_mlp,
            hidden_pre,
            activated,
        ) = saved[layer_idx]
        gain_at = 1 + 4 * layer_idx
        grad_branch = grad_hidden.astype(jnp.bfloat16)
        down_grad = jnp.einsum(
            "tf,td->fd", activated, grad_branch, preferred_element_type=jnp.float32
        )
        grad_act = jnp.einsum(
            "td,fd->tf", grad_branch, down_weight, preferred_element_type=jnp.float32
        )
        _, gelu_pull = jax.vjp(jax.nn.gelu, hidden_pre)
        grad_pre = gelu_pull(grad_act)[0].astype(jnp.bfloat16)
        in_grad = jnp.einsum("td,tf->df", normed_mlp, grad_pre, preferred_element_type=jnp.float32)
        grad_normed_mlp = input_total(
            jnp.einsum("tf,df->td", grad_pre, in_weight, preferred_element_type=jnp.float32)
        )
        _, pullback = jax.vjp(norm_rows, residual, vec_rows[gain_at + 2], vec_rows[gain_at + 3])
        grad_from_norm, vec_grads[gain_at + 2], vec_grads[gain_at + 3] = pullback(grad_normed_mlp)
        grad_residual = grad_hidden + grad_from_norm
        grad_attn = grad_residual.astype(jnp.bfloat16)
        out_grad = jnp.einsum(
            "te,td->ed", mixed_heads, grad_attn, preferred_element_type=jnp.float32
        )
        grad_mixed = jnp.einsum(
            "td,ed->te", grad_attn, out_weight, preferred_element_type=jnp.float32
        )
        grad_mixed = grad_mixed.astype(jnp.bfloat16).reshape(shaped.shape[1:])
        scores = (
            jnp.einsum("bqhd,bkhd->bhqk", shaped[0], shaped[1], preferred_element_type=jnp.float32)
            * score_scale
        )
        attn_probs = jnp.exp(scores - top_log[..., None])
        grad_value = jnp.einsum(
            "bhqk,bqhd->bkhd",
            attn_probs.astype(jnp.bfloat16),
            grad_mixed,
            preferred_element_type=jnp.float32,
        ).astype(jnp.bfloat16)
        grad_probs = jnp.einsum(
            "bqhd,bkhd->bhqk", grad_mixed, shaped[2], preferred_element_type=jnp.float32
        )
        grad_scores = attn_probs * (
            grad_probs - jnp.sum(grad_probs * attn_probs, axis=-1, keepdims=True)
        )
        grad_scores = grad_scores.astype(jnp.bfloat16)
        grad_query = (
            jnp.einsum(
                "bhqk,bkhd->bqhd", grad_scores, shaped[1], preferred_element_type=jnp.float32
            )
            * score_scale
        ).astype(jnp.bfloat16)
        grad_key = (
            jnp.einsum(
                "bhqk,bqhd->bkhd", grad_scores, shaped[0], preferred_element_type=jnp.float32
            )
            * score_scale
        ).astype(jnp.bfloat16)
        grad_qkv = jnp.stack([grad_query, grad_key, grad_value]).reshape(
            3, row_total, qkv_weight.shape[-1]
        )
        qkv_grad = jnp.einsum(
            "td,wte->wde", normed_low, grad_qkv, preferred_element_type=jnp.float32
        )
        grad_normed = input_total(
            jnp.einsum("wte,wde->td", grad_qkv, qkv_weight, preferred_element_type=jnp.float32)
        )
        _, pullback = jax.vjp(norm_rows, hidden_in, vec_rows[gain_at], vec_rows[gain_at + 1])
        grad_from_first, vec_grads[gain_at], vec_grads[gain_at + 1] = pullback(grad_normed)
        grad_hidden = grad_residual + grad_from_first
        layer_grads.insert(0, (qkv_grad, out_grad, in_grad, down_grad))
    grad_hidden = grad_hidden.reshape(conv_out.shape)
    _, gelu_pull = jax.vjp(jax.nn.gelu, conv_out)
    grad_conv = gelu_pull(grad_hidden)[0].astype(jnp.bfloat16)
    grad_groups = grad_conv.reshape(clip_count, frames, GROUPS, GW)
    conv_grad = jnp.stack(
        [
            jnp.einsum(
                "bfgo,bfgi->goi",
                grad_groups,
                padded_low[:, tap : tap + frames],
                preferred_element_type=jnp.float32,
            )
            for tap in range(KERNEL)
        ],
        axis=2,
    )
    padded_grad = pad_frames(grad_conv)
    grad_through = jnp.zeros((clip_count, frames, GROUPS, GW), jnp.float32)
    for tap in range(KERNEL):
        begin = KERNEL - 1 - tap
        grad_through = grad_through + jnp.einsum(
            "bfgo,goi->bfgi",
            padded_grad[:, begin : begin + frames],
            conv_weight[:, :, tap],
            preferred_element_type=jnp.float32,
        )
    grad_embed = grad_hidden + grad_through.reshape(conv_out.shape)
    mask_col = mask_micro[..., None]
    vec_grads[0] = jnp.sum(grad_embed * mask_col, axis=(0, 1))
    grad_proj = (grad_embed * (1.0 - mask_col)).astype(jnp.bfloat16)
    proj_grad = jnp.einsum("bfc,bfd->cd", inputs, grad_proj, preferred_element_type=jnp.float32)
    return (loss_add, (layer_grads, head_grad, proj_grad, conv_grad, jnp.stack(vec_grads)))


def owner_layout(grads, block_slot, slot_total):
    layer_grads, head_grad, proj_grad, conv_grad, vec_grad = grads
    blocks = pack_half(layer_grads, head_grad)
    slot_grads = (
        jnp.zeros((slot_total, 1) + blocks.shape[1:], jnp.float32).at[block_slot, 0].set(blocks)
    )
    channels = conv_grad.shape[0] * conv_grad.shape[1]
    col_grads = jnp.concatenate([proj_grad.T, conv_grad.reshape(channels, -1), vec_grad.T], axis=1)
    return (slot_grads, col_grads)


def local(
    features,
    mask_starts,
    block_slot,
    settings,
    matrices,
    momentum,
    statistics,
    inverse_roots,
    teacher,
    dense_params,
    dense_moment,
    dense_second,
    teacher_dense,
):
    clip_dev = features.shape[0]
    per_micro = clip_dev // MICRO
    frames = features.shape[1]
    slot_total = matrices.shape[0] * lax.axis_size("dp")
    masked_all = span_mask(mask_starts, frames)
    mask_total = lax.psum(jnp.sum(masked_all), "dp")
    loss_scale = 1.0 / (mask_total * math.sqrt(D))
    teach_slots, teach_cols = (
        lax.all_gather(teacher.astype(jnp.bfloat16), "dp", axis=0, tiled=True),
        lax.all_gather(teacher_dense.astype(jnp.bfloat16), "dp", axis=0, tiled=True),
    )
    teach_params = params_of(teach_slots, teach_cols, block_slot)
    loss_part = jnp.zeros((), jnp.float32)
    reduced_slots = None
    reduced_cols = None
    for micro_idx in range(MICRO):
        slots_low, cols_low = (
            lax.all_gather(matrices.astype(jnp.bfloat16), "dp", axis=0, tiled=True),
            lax.all_gather(dense_params.astype(jnp.bfloat16), "dp", axis=0, tiled=True),
        )
        params = params_of(slots_low, cols_low, block_slot)
        inputs = features[micro_idx * per_micro : (micro_idx + 1) * per_micro]
        mask_micro = masked_all[micro_idx * per_micro : (micro_idx + 1) * per_micro]
        _, teach_branches, _ = forward(teach_params, inputs, jnp.zeros_like(mask_micro), False)
        target = teacher_targets(teach_branches, per_micro, frames).reshape(per_micro * frames, D)
        loss_add, grads = student_step(params, inputs, mask_micro, target, loss_scale)
        loss_part = loss_part + loss_add
        slot_part, col_part = owner_layout(grads, block_slot, slot_total)
        slot_sum, col_sum = (
            lax.psum_scatter(slot_part, "dp", scatter_dimension=0, tiled=True),
            lax.psum_scatter(col_part, "dp", scatter_dimension=0, tiled=True),
        )
        if reduced_slots is None:
            reduced_slots, reduced_cols = (slot_sum, col_sum)
        else:
            reduced_slots, reduced_cols = (reduced_slots + slot_sum, reduced_cols + col_sum)
    local_square = jnp.sum(reduced_slots * reduced_slots) + 0.5 * jnp.sum(
        reduced_cols * reduced_cols
    )
    loss_value, square_sum = lax.psum((loss_part, local_square), ("dp", "tensor"))
    grad_norm = jnp.sqrt(square_sum)
    factor = jnp.minimum(1.0, settings[1] / grad_norm)
    clipped = reduced_slots[:, 0] * factor
    left_new = state_decay * statistics[:, 0, 0] + (1.0 - state_decay) * jnp.einsum(
        "sij,skj->sik", clipped, clipped, precision=lax.Precision.HIGHEST
    )
    right_new = state_decay * statistics[:, 0, 1] + (1.0 - state_decay) * jnp.einsum(
        "sji,sjk->sik", clipped, clipped, precision=lax.Precision.HIGHEST
    )
    left_side = jnp.einsum(
        "sij,sjk->sik", inverse_roots[:, 0, 0], clipped, precision=lax.Precision.HIGHEST
    )
    precond = jnp.einsum(
        "sij,sjk->sik", left_side, inverse_roots[:, 0, 1], precision=lax.Precision.HIGHEST
    )
    momentum_new = state_decay * momentum[:, 0] + (1.0 - state_decay) * precond
    matrices_new = matrices[:, 0] - matrix_rate * momentum_new
    teacher_new = settings[0] * teacher[:, 0] + (1.0 - settings[0]) * matrices_new
    statistics_new = jnp.stack([left_new, right_new], axis=1)[:, None]
    grad_small = reduced_cols * factor
    dense_moment_new = state_decay * dense_moment + (1.0 - state_decay) * grad_small
    dense_second_new = state_decay * dense_second + (1.0 - state_decay) * grad_small * grad_small
    dense_new = dense_params - dense_rate * dense_moment_new / (
        jnp.sqrt(dense_second_new) + adam_eps
    )
    teacher_dense_new = settings[0] * teacher_dense + (1.0 - settings[0]) * dense_new
    return (
        loss_value,
        grad_norm,
        matrices_new[:, None],
        momentum_new[:, None],
        statistics_new,
        teacher_new[:, None],
        dense_new,
        dense_moment_new,
        dense_second_new,
        teacher_dense_new,
    )


def solution(mesh):
    return jax.shard_map(
        local,
        mesh=mesh,
        in_specs=(
            P("dp", None, None),
            P("dp", None),
            P(),
            P(),
            P("dp", "tensor", None, None),
            P("dp", "tensor", None, None),
            P("dp", "tensor", None, None, None),
            P("dp", "tensor", None, None, None),
            P("dp", "tensor", None, None),
            P("dp", None),
            P("dp", None),
            P("dp", None),
            P("dp", None),
        ),
        out_specs=(
            P(),
            P(),
            P("dp", "tensor", None, None),
            P("dp", "tensor", None, None),
            P("dp", "tensor", None, None, None),
            P("dp", "tensor", None, None),
            P("dp", None),
            P("dp", None),
            P("dp", None),
            P("dp", None),
        ),
        check_vma=False,
    )
```

profile of v0, /device:TPU:0, one launch (start us, length us, event | category | flops | bytes accessed | tf_op | source)
XLA Modules:
  0.0 1775.7 jit_solution(11368626138858517194)
XLA Ops:
  17.3 38.6 %all-gather.5.cloned.1.call-done = bf16[768,1435]{1,0:T(8,128)(2,1)} async-done(((bf16[48,1435]{1,0:T(8,128)(2,1)}), bf16[768,1435]{1,0:T(8,128)(2,1)}) %all-gather.5.cloned.1.call-update) | async-done | bytes 2204176 | tf_op jit(solution)/shard_map/all_gather | solution.py:417
  63.9 5.3 reshape.2620
  69.5 16.6 fusion.518
  93.1 6.7 all-gather.9.cloned.1.call-done
  101.2 5.1 reshape.2621
  108.7 16.7 fusion.519
  175.3 24.3 %all-gather.7.cloned.1.call-done = bf16[64,1,384,384]{3,2,1,0:T(8,128)(2,1)} async-done(((bf16[4,1,384,384]{3,2,1,0:T(8,128)(2,1)}), bf16[64,1,384,384]{3,2,1,0:T(8,128)(2,1)}) %all-gather.7.cloned.1.call-update) | async-done | bytes 18874384 | tf_op jit(solution)/shard_map/all_gather | solution.py:416
  199.6 14.0 gather_fusion
  213.7 86.9 %all-gather.11.cloned.1.call-done = bf16[64,1,384,384]{3,2,1,0:T(8,128)(2,1)} async-done(((bf16[4,1,384,384]{3,2,1,0:T(8,128)(2,1)}), bf16[64,1,384,384]{3,2,1,0:T(8,128)(2,1)}) %all-gather.11.cloned.1.call-update) | async-done | bytes 18874384 | tf_op jit(solution)/shard_map/all_gather | solution.py:407
  300.6 14.0 gather_fusion.1
  314.6 12.4 broadcast_select_fusion
  327.0 3.9 slice_bitcast_fusion
  334.8 4.4 copy-done.7
  375.5 11.5 fusion.516
  403.0 24.2 %all-reduce.43.cloned.1.call-done = (bf16[256,768]{1,0:T(8,128)(2,1)}, bf16[256,768]{1,0:T(8,128)(2,1)}, bf16[256,768]{1,0:T(8,128)(2,1)}, bf16[256,768]{1,0:T(8,128)(2,1)}) async-done(((bf16[256,768]{1,0:T(8,128)(2,1)}, bf16[256,768]{1,0:T(8,128)(2,1)}, bf16[256,768]{1,0:T(8,128)(2,1)}, bf16[256,768]{1,0:T(8,128)(2,1)}), (bf16[256,768]{1,0:T(8,128)(2,1)}, bf16[256,768]{1,0:T(8,128)(2,1)}, ...) | async-done | bytes 1572880 | tf_op jit(solution)/shard_map/psum | solution.py:141
  439.9 4.9 convolution_convert_fusion.13
  444.8 4.9 convolution_convert_fusion.17
  462.8 38.6 %all-reduce.41.cloned.1.call-done = (bf16[256,768]{1,0:T(8,128)(2,1)}, bf16[256,768]{1,0:T(8,128)(2,1)}, bf16[256,768]{1,0:T(8,128)(2,1)}, bf16[256,768]{1,0:T(8,128)(2,1)}) async-done(((bf16[256,768]{1,0:T(8,128)(2,1)}, bf16[256,768]{1,0:T(8,128)(2,1)}, bf16[256,768]{1,0:T(8,128)(2,1)}, bf16[256,768]{1,0:T(8,128)(2,1)}), (bf16[256,768]{1,0:T(8,128)(2,1)}, bf16[256,768]{1,0:T(8,128)(2,1)}, ...) | async-done | bytes 1572880 | tf_op jit(solution)/shard_map/psum | solution.py:141
  544.7 32.3 %all-reduce.39.cloned.1.call-done = (bf16[256,768]{1,0:T(8,128)(2,1)}, bf16[256,768]{1,0:T(8,128)(2,1)}, bf16[256,768]{1,0:T(8,128)(2,1)}, bf16[256,768]{1,0:T(8,128)(2,1)}) async-done(((bf16[256,768]{1,0:T(8,128)(2,1)}, bf16[256,768]{1,0:T(8,128)(2,1)}, bf16[256,768]{1,0:T(8,128)(2,1)}, bf16[256,768]{1,0:T(8,128)(2,1)}), (bf16[256,768]{1,0:T(8,128)(2,1)}, bf16[256,768]{1,0:T(8,128)(2,1)}, ...) | async-done | bytes 1572880 | tf_op jit(solution)/shard_map/psum | solution.py:141
  589.7 5.2 convolution_convert_fusion.12
  594.8 5.0 convolution_convert_fusion.16
  601.2 33.6 %psum.211 = f32[]{:T(128)} all-reduce(f32[]{:T(128)} %convert_reduce_fusion.14), channel_id=1, replica_groups=mesh['dp'=16,'tensor'=2] {'dp'}, use_global_device_ids=true, to_apply=%region_41.43 | all-reduce | flops 1 | bytes 8 | tf_op jit(solution)/shard_map/psum | solution.py:404
  639.5 12.2 all-reduce.37.cloned.1.call-done
  667.4 28.3 %all-reduce.35.cloned.1.call-done = (bf16[256,768]{1,0:T(8,128)(2,1)}, bf16[256,768]{1,0:T(8,128)(2,1)}) async-done(((bf16[256,768]{1,0:T(8,128)(2,1)}, bf16[256,768]{1,0:T(8,128)(2,1)}), (bf16[256,768]{1,0:T(8,128)(2,1)}, bf16[256,768]{1,0:T(8,128)(2,1)})) %all-reduce.35.cloned.1.call-update) | async-done | bytes 786448 | tf_op jit(solution)/shard_map/psum | solution.py:145
  717.1 6.2 reshape.2413
  723.2 4.8 copy.1321
  728.1 6.7 reshape.2415
  734.8 4.8 copy.1322
  739.7 5.0 fusion.467
  744.7 6.9 reshape.2403
  751.6 4.9 copy.1297
  759.7 6.2 reshape.2401
  765.9 4.8 copy.1296
  833.5 8.5 all-reduce.31.cloned.1.call-done
  862.8 6.2 reshape.2408
  869.0 4.8 copy.1317
  873.8 6.7 reshape.2410
  880.5 4.9 copy.1318
  888.8 6.7 reshape.2398
  895.6 5.0 copy.1293
  903.7 6.4 reshape.2396
  910.1 4.9 copy.1292
  915.0 4.9 all-reduce.29.cloned.1.call-done
  974.8 5.1 constant_dynamic-update-slice_fusion.18
  980.0 5.0 constant_dynamic-update-slice_fusion.17
  996.3 12.6 broadcast.929.clone.1
  1008.9 51.4 %scatter_fusion.1 = f32[64,384,384]{2,1,0:T(8,128)} fusion(f32[64,384,384]{2,1,0:T(8,128)} %broadcast.929.clone.1, s32[50]{0:T(128)S(1)} %copy-done.462, f32[50,384,384]{2,1,0:T(8,128)} %constant_dynamic-update-slice_fusion.11), kind=kCustom, calls=%fused_computation.3 | custom fusion | bytes 88473800 | tf_op jit(solution)/shard_map/scatter | solution.py:377
  1122.9 8.9 copy.1380
  1131.8 7.3 reshape.2472
  1171.3 9.1 copy.1354
  1180.6 7.4 reshape.2439
  1188.3 4.4 maximum_add_fusion
  1192.7 5.9 copy.1491
  1201.2 4.9 constant_dynamic-update-slice_fusion.7
  1206.1 5.2 constant_dynamic-update-slice_fusion.6
  1222.7 12.8 broadcast.929.clone
  1235.5 51.8 %scatter_fusion = f32[64,384,384]{2,1,0:T(8,128)} fusion(f32[64,384,384]{2,1,0:T(8,128)} %broadcast.929.clone, s32[50]{0:T(128)S(1)} %copy-done.463, f32[50,384,384]{2,1,0:T(8,128)} %constant_dynamic-update-slice_fusion), kind=kCustom, calls=%fused_computation.2 | custom fusion | bytes 88473800 | tf_op jit(solution)/shard_map/scatter | solution.py:377
  1287.3 38.3 %add_bitcast_fusion = f32[64,1,384,384]{3,2,0,1:T(8,128)} fusion(f32[64,384,384]{2,1,0:T(8,128)} %scatter_fusion, f32[64,384,384]{2,1,0:T(8,128)} %scatter_fusion.1), kind=kLoop, calls=%fused_computation.4 | loop fusion | flops 9437184 | bytes 113246208 | tf_op jit(solution)/shard_map/add | solution.py:434
  1330.8 359.8 %reduce-scatter.5.cloned.1.call-done = f32[4,1,384,384]{3,2,0,1:T(8,128)} async-done(((f32[64,1,384,384]{3,2,0,1:T(8,128)}), f32[4,1,384,384]{3,2,0,1:T(8,128)}) %reduce-scatter.5.cloned.1.call-update) | async-done | bytes 2359312 | tf_op jit(solution)/shard_map/reduce_scatter | solution.py:428
  1694.8 39.7 %all-reduce.7 = (f32[]{:T(128)}, f32[]{:T(128)}) all-reduce(f32[]{:T(128)S(6)} %multiply.387, f32[]{:T(128)S(6)} %add.1430), channel_id=1, replica_groups=mesh['dp'=16,'tensor'=2] {'dp','tensor'}, use_global_device_ids=true, to_apply=%region_81.83 | all-reduce | flops 2 | bytes 16 | tf_op jit(solution)/shard_map/psum | solution.py:438
  1735.8 6.4 fusion.3
  1742.2 6.4 fusion.1
  1752.7 5.0 fusion.6
  1757.7 4.9 fusion.14
  (1603 shorter events, 538.0 us)
Async XLA Ops:
  7.2 48.7 %all-gather.5.cloned.1.call-start = ((), (), s32[]{:S(2)}) async-start(), calls=%async_computation.2 | async-start | bytes 2506752 | tf_op jit(solution)/shard_map/all_gather | solution.py:417
  8.9 90.9 %all-gather.9.cloned.1.call-start = ((), (), s32[]{:S(2)}) async-start(), calls=%async_computation.4 | async-start | bytes 2506752 | tf_op jit(solution)/shard_map/all_gather | solution.py:408
  10.6 189.0 %all-gather.7.cloned.1.call-start = ((), (), s32[]{:S(2)}) async-start(), calls=%async_computation.3 | async-start | bytes 20054016 | tf_op jit(solution)/shard_map/all_gather | solution.py:416
  13.7 286.9 %all-gather.11.cloned.1.call-start = ((), (), s32[]{:S(2)}) async-start(), calls=%async_computation.5 | async-start | bytes 20054016 | tf_op jit(solution)/shard_map/all_gather | solution.py:407
  14.9 412.3 %all-reduce.43.cloned.1.call-start = ((), (), s32[]{:S(2)}) async-start(), calls=%async_computation.16 | async-start | bytes 3145728 | tf_op jit(solution)/shard_map/psum | solution.py:141
  69.4 23.0 %copy-start = (bf16[1,274,768]{1,2,0:T(8,128)(2,1)}, bf16[1,274,768]{1,2,0:T(8,128)(2,1)S(1)}, u32[]{:S(2)}) copy-start(bf16[1,274,768]{1,2,0:T(8,128)(2,1)S(1)} %pad.22.clone) | copy-start | bytes 1262596
  86.3 59.3 %copy-start.110 = (bf16[16,48,1,48]{3,2,1,0:T(2,128)(2,1)}, bf16[16,48,1,48]{3,2,1,0:T(2,128)(2,1)S(1)}, u32[]{:S(2)}) copy-start(bf16[16,48,1,48]{3,2,1,0:T(2,128)(2,1)S(1)} %get-tuple-element.231) | copy-start | bytes 221188
  93.1 73.3 %copy-start.82 = (f32[256,768]{1,0:T(8,128)}, f32[256,768]{1,0:T(8,128)S(1)}, u32[]{:S(2)}) copy-start(f32[256,768]{1,0:T(8,128)S(1)} %copy.1268) | copy-start | bytes 2359300
  136.4 9.2 copy-start.2
  148.2 21.4 %copy-start.84 = (f32[256,768]{1,0:T(8,128)}, f32[256,768]{1,0:T(8,128)S(1)}, u32[]{:S(2)}) copy-start(f32[256,768]{1,0:T(8,128)S(1)} %copy.1208) | copy-start | bytes 2359300
  168.5 258.7 %copy-start.19 = (f32[256,768]{1,0:T(8,128)}, f32[256,768]{1,0:T(8,128)S(1)}, u32[]{:S(2)}) copy-start(f32[256,768]{1,0:T(8,128)S(1)} %get-tuple-element.197) | copy-start | bytes 2359300
  168.6 174.2 %copy-start.377 = (f32[256]{0:T(256)}, f32[256]{0:T(256)S(1)}, u32[]{:S(2)}) copy-start(f32[256]{0:T(256)S(1)} %broadcast_multiply_fusion.12) | copy-start | bytes 3076
  171.1 258.6 %copy-start.21 = (f32[256,768]{1,0:T(8,128)}, f32[256,768]{1,0:T(8,128)S(1)}, u32[]{:S(2)}) copy-start(f32[256,768]{1,0:T(8,128)S(1)} %get-tuple-element.201) | copy-start | bytes 2359300
  171.1 191.1 %copy-start.379 = (f32[256]{0:T(256)}, f32[256]{0:T(256)S(1)}, u32[]{:S(2)}) copy-start(f32[256]{0:T(256)S(1)} %broadcast_multiply_fusion.21) | copy-start | bytes 3076
  174.6 180.6 %copy-start.470 = (f32[768]{0:T(1024)}, f32[768]{0:T(1024)S(1)}, u32[]{:S(2)}) copy-start(f32[768]{0:T(1024)S(1)} %get-tuple-element.126) | copy-start | bytes 9220
  174.6 180.6 %copy-start.472 = (f32[768]{0:T(1024)}, f32[768]{0:T(1024)S(1)}, u32[]{:S(2)}) copy-start(f32[768]{0:T(1024)S(1)} %get-tuple-element.127) | copy-start | bytes 9220
  174.7 168.1 %copy-start.399 = (f32[256]{0:T(256)}, f32[256]{0:T(256)S(1)}, u32[]{:S(2)}) copy-start(f32[256]{0:T(256)S(1)} %fusion.434) | copy-start | bytes 3076
  174.7 187.5 %copy-start.401 = (f32[256]{0:T(256)}, f32[256]{0:T(256)S(1)}, u32[]{:S(2)}) copy-start(f32[256]{0:T(256)S(1)} %fusion.429) | copy-start | bytes 3076
  300.6 14.0 copy-start.486
  327.0 12.2 copy-start.7
  345.0 20.5 %copy-start.227 = (bf16[1,256,384]{1,2,0:T(8,128)(2,1)}, bf16[1,256,384]{1,2,0:T(8,128)(2,1)S(1)}, u32[]{:S(2)}) copy-start(bf16[1,256,384]{1,2,0:T(8,128)(2,1)S(1)} %get-tuple-element.295) | copy-start | bytes 589828
  346.1 19.4 %copy-start.8 = (f32[6,256,256]{1,2,0:T(8,128)}, f32[6,256,256]{1,2,0:T(8,128)S(1)}, u32[]{:S(2)}) copy-start(f32[6,256,256]{1,2,0:T(8,128)S(1)} %get-tuple-element.359) | copy-start | bytes 4718596
  346.4 19.1 %copy-start.344 = (f32[6,256]{1,0:T(8,128)}, f32[6,256]{1,0:T(8,128)S(1)}, u32[]{:S(2)}) copy-start(f32[6,256]{1,0:T(8,128)S(1)} %log_add_fusion.3) | copy-start | bytes 18436
  375.5 126.0 %all-reduce.41.cloned.1.call-start = ((), (), s32[]{:S(2)}) async-start(), calls=%async_computation.15 | async-start | bytes 3145728 | tf_op jit(solution)/shard_map/psum | solution.py:141
  403.0 25.7 %copy-start.38 = (f32[256,768]{1,0:T(8,128)S(1)}, f32[256,768]{1,0:T(8,128)}, u32[]{:S(2)}) copy-start(f32[256,768]{1,0:T(8,128)} %copy-done.37) | copy-start | bytes 2359300
  429.9 80.8 %copy-start.4 = (f32[256,768]{1,0:T(8,128)}, f32[256,768]{1,0:T(8,128)S(1)}, u32[]{:S(2)}) copy-start(f32[256,768]{1,0:T(8,128)S(1)} %get-tuple-element.195) | copy-start | bytes 2359300
  449.7 127.3 %all-reduce.39.cloned.1.call-start = ((), (), s32[]{:S(2)}) async-start(), calls=%async_computation.14 | async-start | bytes 3145728 | tf_op jit(solution)/shard_map/psum | solution.py:141
  461.8 41.1 %copy-start.352 = (f32[768]{0:T(1024)S(1)}, f32[768]{0:T(1024)}, u32[]{:S(2)}) copy-start(f32[768]{0:T(1024)} %get-tuple-element.114) | copy-start | bytes 9220
  461.8 41.1 %copy-start.373 = (f32[768]{0:T(1024)S(1)}, f32[768]{0:T(1024)}, u32[]{:S(2)}) copy-start(f32[768]{0:T(1024)} %get-tuple-element.113) | copy-start | bytes 9220
  462.8 40.0 %copy-start.327 = (bf16[1,768,384]{1,2,0:T(8,128)(2,1)S(1)}, bf16[1,768,384]{1,2,0:T(8,128)(2,1)}, u32[]{:S(2)}) copy-start(bf16[1,768,384]{1,2,0:T(8,128)(2,1)} %copy.1466) | copy-start | bytes 1769476
  505.0 9.1 copy-start.241
  505.5 8.7 copy-start.12
  525.2 126.4 %all-reduce.37.cloned.1.call-start = ((), (), s32[]{:S(2)}) async-start(), calls=%async_computation.13 | async-start | bytes 3145728 | tf_op jit(solution)/shard_map/psum | solution.py:141
  544.7 33.8 %copy-start.59 = (f32[256,768]{1,0:T(8,128)S(1)}, f32[256,768]{1,0:T(8,128)}, u32[]{:S(2)}) copy-start(f32[256,768]{1,0:T(8,128)} %copy-done.58) | copy-start | bytes 2359300
  599.9 95.8 %all-reduce.35.cloned.1.call-start = ((), (), s32[]{:S(2)}) async-start(), calls=%async_computation.12 | async-start | bytes 1572864 | tf_op jit(solution)/shard_map/psum | solution.py:145
  661.2 113.0 %all-reduce.33.cloned.1.call-start = ((), (), s32[]{:S(2)}) async-start(), calls=%async_computation.11 | async-start | bytes 1572864 | tf_op jit(solution)/shard_map/psum | solution.py:145
  665.8 29.9 %copy-start.364 = (f32[768]{0:T(1024)S(1)}, f32[768]{0:T(1024)}, u32[]{:S(2)}) copy-start(f32[768]{0:T(1024)} %get-tuple-element.109) | copy-start | bytes 9220
  665.8 29.9 %copy-start.388 = (f32[256]{0:T(256)S(1)}, f32[256]{0:T(256)}, u32[]{:S(2)}) copy-start(f32[256]{0:T(256)} %copy-done.387) | copy-start | bytes 3076
  665.8 29.9 %copy-start.391 = (f32[256]{0:T(256)S(1)}, f32[256]{0:T(256)}, u32[]{:S(2)}) copy-start(f32[256]{0:T(256)} %copy-done.389) | copy-start | bytes 3076
  665.8 29.9 %copy-start.409 = (f32[256]{0:T(256)S(1)}, f32[256]{0:T(256)}, u32[]{:S(2)}) copy-start(f32[256]{0:T(256)} %copy-done.408) | copy-start | bytes 3076
  665.8 29.9 %copy-start.412 = (f32[256]{0:T(256)S(1)}, f32[256]{0:T(256)}, u32[]{:S(2)}) copy-start(f32[256]{0:T(256)} %copy-done.410) | copy-start | bytes 3076
  667.4 30.8 %copy-start.460 = (f32[256]{0:T(256)S(1)}, f32[256]{0:T(256)}, u32[]{:S(2)}) copy-start(f32[256]{0:T(256)} %copy-done.459) | copy-start | bytes 3076
  667.4 30.8 %copy-start.458 = (f32[256]{0:T(256)S(1)}, f32[256]{0:T(256)}, u32[]{:S(2)}) copy-start(f32[256]{0:T(256)} %copy-done.457) | copy-start | bytes 3076
  698.9 11.8 copy-start.76
  739.6 102.3 %all-reduce.31.cloned.1.call-start = ((), (), s32[]{:S(2)}) async-start(), calls=%async_computation.10 | async-start | bytes 1572864 | tf_op jit(solution)/shard_map/psum | solution.py:145
  807.4 112.5 %all-reduce.29.cloned.1.call-start = ((), (), s32[]{:S(2)}) async-start(), calls=%async_computation.9 | async-start | bytes 1572864 | tf_op jit(solution)/shard_map/psum | solution.py:145
  829.8 12.1 copy-start.383
  832.5 11.1 copy-start.452
  832.5 11.1 copy-start.450
  832.5 11.1 copy-start.405
  845.5 11.9 copy-start.80
  885.4 178.9 %all-reduce.27.cloned.1.call-start = ((), (), s32[]{:S(2)}) async-start(), calls=%async_computation.8 | async-start | bytes 1572864 | tf_op jit(solution)/shard_map/psum | solution.py:145
  970.2 357.9 %reduce-scatter.7.cloned.1.call-start = ((), (), s32[]{:S(2)}) async-start(), calls=%async_computation.7 | async-start | bytes 5013504 | tf_op jit(solution)/shard_map/reduce_scatter | solution.py:429
  974.8 15.4 slice-start.4
  980.0 8.9 copy-start.236
  980.0 8.9 copy-start.253
  980.0 10.2 slice-start.5
  996.3 12.6 copy-start.462
  1008.9 51.4 %copy-start.103 = (f32[1,768,384]{2,1,0:T(8,128)S(1)}, f32[1,768,384]{2,1,0:T(8,128)}, u32[]{:S(2)}) copy-start(f32[1,768,384]{2,1,0:T(8,128)} %copy.1475) | copy-start | bytes 3538948
  1198.7 491.8 %reduce-scatter.5.cloned.1.call-start = ((), (), s32[]{:S(2)}) async-start(), calls=%async_computation.6 | async-start | bytes 40108032 | tf_op jit(solution)/shard_map/reduce_scatter | solution.py:428
  1201.2 15.5 slice-start.2
  1206.1 10.5 slice-start.3
  1222.7 12.8 copy-start.463
  1690.5 45.3 %copy-start.23 = (f32[4,1,384,384]{3,2,0,1:T(8,128)S(1)}, f32[4,1,384,384]{3,2,0,1:T(8,128)}, u32[]{:S(2)}) copy-start(f32[4,1,384,384]{3,2,0,1:T(8,128)} %reduce-scatter.5.cloned.1.call-done) | copy-start | bytes 7077892
  (450 other events, 1158.4 us)
Sparse Core Ops, SparseCore 0:
  10.8 45.0 all-gather.4
  58.8 41.0 all-gather.8
  102.0 97.6 all-gather.6
  201.7 98.8 all-gather.10
  375.6 51.5 all-reduce.42
  449.8 51.5 all-reduce.40
  525.4 51.5 all-reduce.38
  600.0 51.5 all-reduce.36
  661.3 34.3 all-reduce.34
  739.7 34.3 all-reduce.32
  807.5 34.3 all-reduce.30
  885.5 34.3 all-reduce.28
  970.3 34.3 all-reduce.26
  1198.8 75.6 reduce-scatter.6
  1325.7 364.8 reduce-scatter.4
where the time goes:
time: 1780 us
  waiting for transfers between devices  669 us (38%)
  local copies, waits for them, and re-layouts  601 us (34%)
  matrix products  274 us (15%)
  other arithmetic  130 us (7%)
  blocking collectives  73.3 us (4%)
  between operations  26.6 us (1%)
    reduce_scatter x1, waiting for transfers between devices, local(): lax.psum_scatter(slot_part, 'dp', scatter_dimension=0, tiled=True)  360 us
    unnamed x1033, local copies, waits for them, and re-layouts  133 us
    psum x4, waiting for transfers between devices, branch_total(): lax.psum(partial_value.astype(jnp.bfloat16), 'tensor').astype(jnp.float32)  107 us
    scatter x2, local copies, waits for them, and re-layouts, owner_layout(): jnp.zeros((slot_total, 1) + blocks.shape[1:], jnp.float32).at[block_slot, 0]  103 us
    all_gather x1, waiting for transfers between devices, local(): lax.all_gather(teacher.astype(jnp.bfloat16), 'dp', axis=0, tiled=True)  86.9 us
    reshape x8, local copies, waits for them, and re-layouts, untile(): matrix.reshape(row_count, BLK, col_count, BLK).transpose(0, 2, 1, 3)  52 us
    psum x5, waiting for transfers between devices, input_total(): lax.psum(partial_value.astype(jnp.bfloat16), 'tensor').astype(jnp.float32)  45.1 us
    dot_general x38, matrix products, student_step(): jnp.einsum('bfgo,bfgi->goi', grad_groups, padded_low[:, tap:tap + frames]...  41.2 us
  transfers between devices with their start and end apart: 15, of which 13 were waited for; matrix products, arithmetic and copies ran while one was open for 28% of the time, Pallas kernels for 0%

commit v1 on v0

v1 whole, which is shorter than its diff:
```python
import functools
import math

import jax
import jax.numpy as jnp
from jax import lax
from jax.experimental import pallas as pl
from jax.experimental.pallas import tpu as pltpu
from jax.sharding import PartitionSpec as P

D = 768
HD = 64
FF = 3072
C = 512
KERNEL = 19
GROUPS = 16
LAYERS = 2
MASK_LEN = 10
BLK = 384
GW = 48
F = 256
NBLK = 24 * LAYERS + 2
CONV = KERNEL * GW
CONV_PAD = 1024
VEC_AT = C + CONV_PAD
WIDE = VEC_AT + 128
NVEC = 3 + 4 * LAYERS
MARGIN = KERNEL // 2
COUNT_AT = 16
COUNT_BASE = 16.0

norm_eps = 1e-05
loss_beta = 0.25
state_decay = 0.5
matrix_rate = 1.0
dense_rate = 0.01
adam_eps = 1e-08
f32 = jnp.float32
bf16 = jnp.bfloat16
VLIM = 60 * 2**20
C0 = math.sqrt(2.0 / math.pi)
C1 = 0.044715
ANY = pl.BlockSpec(memory_space=pl.ANY)


def nn(a, b):
    return lax.dot_general(a, b, (((1,), (0,)), ((), ())), preferred_element_type=f32)


def nt(a, b):
    return lax.dot_general(a, b, (((1,), (1,)), ((), ())), preferred_element_type=f32)


def tn(a, b):
    return lax.dot_general(a, b, (((0,), (0,)), ((), ())), preferred_element_type=f32)


def normed(values):
    center = values - jnp.mean(values, axis=-1, keepdims=True)
    spread = lax.rsqrt(jnp.mean(center * center, axis=-1, keepdims=True) + norm_eps)
    return center * spread, spread


def norm_back(grad, hat, spread, gain):
    scaled = grad * gain
    inner = scaled - jnp.mean(scaled, axis=-1, keepdims=True)
    inner = inner - hat * jnp.mean(scaled * hat, axis=-1, keepdims=True)
    return spread * inner


def gelu_tanh(z):
    return jnp.tanh(C0 * (z + C1 * (z * z * z)))


def gelu(z):
    return 0.5 * z * (1.0 + gelu_tanh(z))


def gelu_both(z):
    th = gelu_tanh(z)
    value = 0.5 * z * (1.0 + th)
    slope = 0.5 * (1.0 + th) + 0.5 * z * (1.0 - th * th) * (C0 * (1.0 + 3.0 * C1 * (z * z)))
    return value, slope


def head_masks():
    lane = lax.broadcasted_iota(jnp.int32, (1, 2 * HD), 1)
    first = jnp.where(lane < HD, 1.0, 0.0).astype(f32)
    return first.astype(bf16), (1.0 - first).astype(bf16), first


def softmax_rows(scores):
    e = jnp.exp(scores - jnp.max(scores, axis=-1, keepdims=True))
    return e * (1.0 / jnp.sum(e, axis=-1, keepdims=True))


def window_rows(emb_ref, g, win_ref, flip):
    rows = emb_ref[pl.ds(pl.multiple_of(g * GW, GW), GW), :]
    lane = lax.broadcasted_iota(jnp.int32, (GW, F), 1)
    for tap in range(KERNEL):
        off = tap - MARGIN if not flip else MARGIN - tap
        moved = rows if off == 0 else pltpu.roll(rows, (-off) % F, 1)
        if off > 0:
            moved = jnp.where(lane < F - off, moved, 0.0)
        elif off < 0:
            moved = jnp.where(lane >= -off, moved, 0.0)
        win_ref[tap * GW : (tap + 1) * GW, :] = moved.astype(bf16)


def front_kernel(keep, w_ref, feat_ref, mask_ref, *refs):
    if keep:
        x_ref, emb_ref, conv_ref, low_s, win_s = refs
    else:
        x_ref, emb_ref, conv_ref, low_s, win_s = (refs[0],) + refs[1:]
    proj = nt(w_ref[:, :C], feat_ref[...])
    if keep:
        vec = w_ref[:, VEC_AT : VEC_AT + 128].astype(f32)
        lane = lax.broadcasted_iota(jnp.int32, (1, 128), 1)
        col = jnp.sum(jnp.where(lane == 0, vec, 0.0), axis=1, keepdims=True)
        proj = jnp.where(mask_ref[...] > 0, col, proj)
    emb_ref[...] = proj
    low_s[...] = proj.astype(bf16).astype(f32)
    win_s[CONV:, :] = jnp.zeros((CONV_PAD - CONV, F), bf16)

    def group(g, carry):
        window_rows(low_s, g, win_s, False)
        rows = pl.ds(pl.multiple_of(g * GW, GW), GW)
        conv_ref[rows, :] = nn(w_ref[rows, C : C + CONV_PAD], win_s[...])
        return carry

    lax.fori_loop(0, GROUPS, group, 0)
    x_ref[...] = (emb_ref[...] + gelu(conv_ref[...])).T


def front(dense_low, feat, mask_row, keep):
    big = jax.ShapeDtypeStruct((D, F), f32)
    vm = pl.BlockSpec(memory_space=pltpu.VMEM)
    scratch = [pltpu.VMEM((D, F), f32), pltpu.VMEM((CONV_PAD, F), bf16)]
    if keep:
        outs, specs = (jax.ShapeDtypeStruct((F, D), f32), big, big), (vm, vm, vm)
    else:
        outs, specs = jax.ShapeDtypeStruct((F, D), f32), vm
        scratch = [pltpu.VMEM((D, F), f32), pltpu.VMEM((D, F), f32)] + scratch
    return pl.pallas_call(
        functools.partial(front_kernel, keep),
        out_shape=outs,
        in_specs=[vm, vm, vm],
        out_specs=specs,
        scratch_shapes=scratch,
        compiler_params=pltpu.CompilerParams(vmem_limit_bytes=VLIM),
    )(dense_low, feat, mask_row)


def front_back_kernel(
    w_ref, feat_ref, mask_ref, dx_ref, emb_ref, conv_ref, vec_ref, out_ref, low_s, dcv_s, dem_s, win_s
):
    grad_x = dx_ref[...].T
    _, slope = gelu_both(conv_ref[...])
    dcv_s[...] = (slope * grad_x).astype(bf16)
    low_s[...] = emb_ref[...].astype(bf16).astype(f32)
    win_s[CONV:, :] = jnp.zeros((CONV_PAD - CONV, F), bf16)
    lane = lax.broadcasted_iota(jnp.int32, (GW, F), 1)

    def group(g, carry):
        rows = pl.ds(pl.multiple_of(g * GW, GW), GW)
        window_rows(low_s, g, win_s, False)
        grad = dcv_s[rows, :]
        out_ref[rows, C : C + CONV_PAD] = nt(grad, win_s[...]).astype(out_ref.dtype)
        spread = tn(w_ref[rows, C : C + CONV_PAD], grad)
        total = jnp.zeros((GW, F), f32)
        for tap in range(KERNEL):
            off = tap - MARGIN
            part = spread[tap * GW : (tap + 1) * GW, :]
            moved = part if off == 0 else pltpu.roll(part, off % F, 1)
            if off > 0:
                moved = jnp.where(lane >= off, moved, 0.0)
            elif off < 0:
                moved = jnp.where(lane < F + off, moved, 0.0)
            total = total + moved
        dem_s[rows, :] = total
        return carry

    lax.fori_loop(0, GROUPS, group, 0)
    grad_emb = grad_x + dem_s[...]
    mask = mask_ref[...]
    mask_grad = jnp.sum(grad_emb * mask, axis=1, keepdims=True)
    grad_proj = (grad_emb * (1.0 - mask)).astype(bf16)
    out_ref[:, :C] = nn(grad_proj, feat_ref[...]).astype(out_ref.dtype)
    vec_t = vec_ref[...].T
    at = lax.broadcasted_iota(jnp.int32, (1, 128), 1)
    out_ref[:, VEC_AT:] = jnp.where(at == 0, mask_grad, vec_t).astype(out_ref.dtype)


def front_back(dense_low, feat, mask_row, grad_x, emb, conv_out, vec_grads):
    vm = pl.BlockSpec(memory_space=pltpu.VMEM)
    return pl.pallas_call(
        front_back_kernel,
        out_shape=jax.ShapeDtypeStruct((D, WIDE), bf16),
        in_specs=[vm] * 7,
        out_specs=vm,
        scratch_shapes=[
            pltpu.VMEM((D, F), f32),
            pltpu.VMEM((D, F), bf16),
            pltpu.VMEM((D, F), f32),
            pltpu.VMEM((CONV_PAD, F), bf16),
        ],
        compiler_params=pltpu.CompilerParams(vmem_limit_bytes=VLIM),
    )(dense_low, feat, mask_row, grad_x, emb, conv_out, vec_grads)


def weight_plan():
    plan = []
    for w in range(3):
        for t in range(2):
            for r in range(2):
                plan.append((t, w * 2 + r, 0, w * 2 + t, r))
    for t in range(2):
        for c in range(2):
            plan.append((t, 6 + c, 1, t, c))
    for cc in range(8):
        t, c = divmod(cc, 4)
        for r in range(2):
            plan.append((t, 8 + r * 4 + c, 2, cc, r))
    for cc in range(8):
        t, r = divmod(cc, 4)
        for c in range(2):
            plan.append((t, 16 + r * 2 + c, 3, cc, c))
    return plan


def block_view(refs, which, at, part):
    ref = refs[which]
    if which in (0, 2):
        return ref.at[at, pl.ds(part * BLK, BLK), :]
    return ref.at[at, :, pl.ds(part * BLK, BLK)]


def start_weights(tab, layer, w_hbm, refs, sem):
    for k, (t, off, which, at, part) in enumerate(weight_plan()):
        src = tab[t * NBLK + layer * 24 + off]
        pltpu.make_async_copy(w_hbm.at[src], block_view(refs, which, at, part), sem.at[k]).start()


def wait_weights(w_hbm, refs, sem, ks):
    plan = weight_plan()
    for k in ks:
        _, _, which, at, part = plan[k]
        pltpu.make_async_copy(w_hbm.at[0], block_view(refs, which, at, part), sem.at[k]).wait()


def wait_mlp(w_hbm, refs, sem, cc):
    for which, base in ((2, 16), (3, 32)):
        for part in range(2):
            pltpu.make_async_copy(
                w_hbm.at[0], block_view(refs, which, cc, part), sem.at[base + cc * 2 + part]
            ).wait()


WEIGHTS = [
    ((6, D, BLK), bf16),
    ((2, BLK, D), bf16),
    ((8, D, BLK), bf16),
    ((8, BLK, D), bf16),
]


def encoder_kernel(keep, tab, x_ref, vec_ref, w_hbm, *refs):
    if keep:
        out_ref, xin_ref, qkv_ref, o_ref, h_ref, z_ref = refs[:6]
        xs, acc, wq, wo, wi, wd, sem = refs[6:]
    else:
        out_ref = refs[0]
        xs, acc, wq, wo, wi, wd, sem, qkv_s, o_s = refs[1:]
    layer = pl.program_id(0)
    buf = lax.rem(layer, 2)
    nxt = lax.rem(layer + 1, 2)

    def weights(b):
        return [wq.at[b], wo.at[b], wi.at[b], wd.at[b]]

    @pl.when(layer == 0)
    def _():
        start_weights(tab, 0, w_hbm, weights(0), sem.at[0])
        xs[...] = x_ref[...]

    @pl.when(layer + 1 < LAYERS)
    def _():
        start_weights(tab, layer + 1, w_hbm, weights(nxt), sem.at[nxt])

    mine, msem = weights(buf), sem.at[buf]
    if keep:
        qkv, o_all = qkv_ref.at[0], o_ref.at[0]
        xin_ref[0] = xs[...]
    else:
        qkv, o_all = qkv_s, o_s
    hat, _ = normed(xs[...])
    a_low = (hat * vec_ref[0, 0:1, :] + vec_ref[0, 1:2, :]).astype(bf16)
    wait_weights(w_hbm, mine, msem, range(16))
    m0, m1, first = head_masks()

    def half(t, carry):
        for w in range(3):
            qkv[w * 2 + t] = nn(a_low, wq[buf, w * 2 + t]).astype(bf16)
        for j in range(3):
            cols = slice(j * 2 * HD, (j + 1) * 2 * HD)
            q, k, v = qkv[t, :, cols], qkv[2 + t, :, cols], qkv[4 + t, :, cols]
            parts = []
            for m in (m0, m1):
                p = softmax_rows(nt(q * m, k) * 0.125)
                parts.append(nn(p.astype(bf16), v))
            o_all[t, :, cols] = jnp.where(first > 0, parts[0], parts[1]).astype(bf16)
        return carry

    lax.fori_loop(0, 2, half, 0)
    h = xs[...] + nn(o_all[0], wo[buf, 0]) + nn(o_all[1], wo[buf, 1])
    xs[...] = h
    if keep:
        h_ref[0] = h
    hat, _ = normed(h)
    c_low = (hat * vec_ref[0, 2:3, :] + vec_ref[0, 3:4, :]).astype(bf16)
    acc[...] = jnp.zeros_like(acc)

    def mlp(cc, carry):
        wait_mlp(w_hbm, mine, msem, cc)
        z = nn(c_low, wi[buf, cc])
        if keep:
            z_ref[0, cc] = z
        acc[...] += nn(gelu(z).astype(bf16), wd[buf, cc])
        return carry

    lax.fori_loop(0, 8, mlp, 0)
    y = acc[...]
    xs[...] = xs[...] + y
    if keep:
        out_ref[...] = xs[...]
    else:
        center = y - jnp.mean(y, axis=0, keepdims=True)
        unit = center * lax.rsqrt(jnp.mean(center * center, axis=0, keepdims=True) + norm_eps)
        unit = unit * (1.0 / LAYERS)

        @pl.when(layer == 0)
        def _():
            out_ref[...] = unit

        @pl.when(layer > 0)
        def _():
            out_ref[...] = out_ref[...] + unit


def encoder(tab, x, vecs, slots, keep):
    whole = pl.BlockSpec((F, D), lambda l, tab: (0, 0))
    per = lambda *s: pl.BlockSpec((1,) + s, lambda l, tab: (l,) + (0,) * len(s))
    outs = [jax.ShapeDtypeStruct((F, D), f32)]
    out_specs = [whole]
    scratch = [pltpu.VMEM((F, D), f32), pltpu.VMEM((F, D), f32)]
    scratch += [pltpu.VMEM((2,) + s, d) for s, d in WEIGHTS]
    scratch += [pltpu.SemaphoreType.DMA((2, 48))]
    if keep:
        for s, d in (
            ((F, D), f32),
            ((6, F, BLK), bf16),
            ((2, F, BLK), bf16),
            ((F, D), f32),
            ((8, F, BLK), f32),
        ):
            outs.append(jax.ShapeDtypeStruct((LAYERS,) + s, d))
            out_specs.append(per(*s))
    else:
        scratch += [pltpu.VMEM((6, F, BLK), bf16), pltpu.VMEM((2, F, BLK), bf16)]
    return pl.pallas_call(
        functools.partial(encoder_kernel, keep),
        out_shape=outs,
        grid_spec=pltpu.PrefetchScalarGridSpec(
            num_scalar_prefetch=1,
            grid=(LAYERS,),
            in_specs=[whole, per(8, D), ANY],
            out_specs=out_specs,
            scratch_shapes=scratch,
        ),
        compiler_params=pltpu.CompilerParams(
            dimension_semantics=("arbitrary",), vmem_limit_bytes=VLIM
        ),
    )(tab, x, vecs, slots)


def head_kernel(
    tab, x_ref, vec_ref, target_ref, mask_ref, scale_ref, w_hbm, dx_ref, grad_ref, vg_ref, loss_ref, wh, sem
):
    copies = []
    for t in range(2):
        for r in range(2):
            src = tab[t * NBLK + 24 * LAYERS + r]
            copies.append(
                pltpu.make_async_copy(
                    w_hbm.at[src], wh.at[t, pl.ds(r * BLK, BLK), :], sem.at[t * 2 + r]
                )
            )
            copies[-1].start()
    hat, spread = normed(x_ref[...])
    gain = vec_ref[0:1, :]
    low = (hat * gain + vec_ref[1:2, :]).astype(bf16)
    row_mask = mask_ref[...]
    scale = scale_ref[0, 0]
    for c in copies:
        c.wait()
    total = jnp.zeros((F, 1), f32)
    grad = jnp.zeros((F, D), f32)
    for t in range(2):
        mismatch = nn(low, wh[t]) - target_ref[:, t * BLK : (t + 1) * BLK]
        size = jnp.abs(mismatch)
        penalty = jnp.where(
            size < loss_beta, 0.5 * mismatch * mismatch / loss_beta, size - 0.5 * loss_beta
        )
        total = total + jnp.sum(penalty, axis=1, keepdims=True) * row_mask
        back = (row_mask * jnp.clip(mismatch / loss_beta, -1.0, 1.0) * scale).astype(bf16)
        weight_grad = tn(low, back).astype(bf16)
        for r in range(2):
            grad_ref[t * 2 + r] = weight_grad[r * BLK : (r + 1) * BLK, :]
        grad = grad + nt(back, wh[t])
    loss_ref[...] = jnp.broadcast_to(jnp.sum(total, axis=0, keepdims=True) * scale, (8, 128))
    vg_ref[0:1, :] = jnp.sum(grad * hat, axis=0, keepdims=True)
    vg_ref[1:2, :] = jnp.sum(grad, axis=0, keepdims=True)
    dx_ref[...] = norm_back(grad, hat, spread, gain)


def head(tab, x, vec, target, mask_col, scale, slots):
    whole = lambda *s: pl.BlockSpec(s, lambda i, tab: (0,) * len(s))
    return pl.pallas_call(
        head_kernel,
        out_shape=[
            jax.ShapeDtypeStruct((F, D), f32),
            jax.ShapeDtypeStruct((4, BLK, BLK), bf16),
            jax.ShapeDtypeStruct((8, D), f32),
            jax.ShapeDtypeStruct((8, 128), f32),
        ],
        grid_spec=pltpu.PrefetchScalarGridSpec(
            num_scalar_prefetch=1,
            grid=(1,),
            in_specs=[
                whole(F, D),
                whole(8, D),
                whole(F, D),
                whole(F, 1),
                pl.BlockSpec(memory_space=pltpu.SMEM),
                ANY,
            ],
            out_specs=[whole(F, D), whole(4, BLK, BLK), whole(8, D), whole(8, 128)],
            scratch_shapes=[pltpu.VMEM((2, D, BLK), bf16), pltpu.SemaphoreType.DMA((4,))],
        ),
        compiler_params=pltpu.CompilerParams(vmem_limit_bytes=VLIM),
    )(tab, x, vec, target, mask_col, scale, slots)


def back_kernel(
    slot_total,
    tab,
    used,
    dx_ref,
    vec_ref,
    xin_ref,
    qkv_ref,
    o_ref,
    h_ref,
    z_ref,
    head_ref,
    w_hbm,
    out_ref,
    grads_hbm,
    vg_ref,
    dxs,
    acc,
    stage,
    zero,
    dqkv,
    wq,
    wo,
    wi,
    wd,
    sem,
    gsem,
    hsem,
    zsem,
):
    step = pl.program_id(0)
    layer = LAYERS - 1 - step
    mine = [wq, wo, wi, wd]
    start_weights(tab, layer, w_hbm, mine, sem)
    plan = weight_plan()

    def head_copy(i):
        dst = tab[(i // 2) * NBLK + 24 * LAYERS + i % 2]
        return pltpu.make_async_copy(head_ref.at[i], grads_hbm.at[dst], hsem.at[i])

    half_slots = slot_total // 2

    def zero_copy(s, t):
        at = used[slot_total // 2 + s] + t * used[2 * (slot_total // 2)]
        return pltpu.make_async_copy(zero, grads_hbm.at[at], zsem.at[s, t])

    @pl.when(step == 0)
    def _():
        dxs[...] = dx_ref[...]
        zero[...] = jnp.zeros_like(zero)
        for i in range(4):
            head_copy(i).start()

        def fill(s, carry):
            @pl.when(used[s] == 0)
            def _():
                zero_copy(s, 0).start()
                zero_copy(s, 1).start()

            return carry

        lax.fori_loop(0, half_slots, fill, 0)

    def grad_copy(k, dst):
        return pltpu.make_async_copy(stage.at[k], grads_hbm.at[dst], gsem.at[k])

    def send(k, off, t):
        grad_copy(k, tab[t * NBLK + layer * 24 + off]).start()

    low = dxs[...].astype(bf16)
    hat2, spread2 = normed(h_ref[0])
    c_low = (hat2 * vec_ref[0, 2:3, :] + vec_ref[0, 3:4, :]).astype(bf16)
    acc[...] = jnp.zeros_like(acc)

    def mlp(cc, carry):
        t, c = lax.div(cc, 4), lax.rem(cc, 4)
        wait_mlp(w_hbm, mine, sem, cc)
        value, slope = gelu_both(z_ref[0, cc])
        grad = (slope * nt(low, wd[cc])).astype(bf16)
        down = tn(value.astype(bf16), low).astype(bf16)
        for part in range(2):
            stage[32 + cc * 2 + part] = down[:, part * BLK : (part + 1) * BLK]
            send(32 + cc * 2 + part, 16 + c * 2 + part, t)
        up = tn(c_low, grad).astype(bf16)
        for part in range(2):
            stage[16 + cc * 2 + part] = up[part * BLK : (part + 1) * BLK, :]
            send(16 + cc * 2 + part, 8 + part * 4 + c, t)
        acc[...] += nt(grad, wi[cc])
        return carry

    lax.fori_loop(0, 8, mlp, 0)
    grad = acc[...]
    vg_ref[0, 2:3, :] = jnp.sum(grad * hat2, axis=0, keepdims=True)
    vg_ref[0, 3:4, :] = jnp.sum(grad, axis=0, keepdims=True)
    grad_h = dxs[...] + norm_back(grad, hat2, spread2, vec_ref[0, 2:3, :])
    dxs[...] = grad_h
    low_h = grad_h.astype(bf16)
    hat1, spread1 = normed(xin_ref[0])
    a_low = (hat1 * vec_ref[0, 0:1, :] + vec_ref[0, 1:2, :]).astype(bf16)
    acc[...] = jnp.zeros_like(acc)
    wait_weights(w_hbm, mine, sem, range(16))
    m0, m1, _ = head_masks()

    def half(t, carry):
        out_grad = tn(o_ref[0, t], low_h).astype(bf16)
        for part in range(2):
            stage[12 + t * 2 + part] = out_grad[:, part * BLK : (part + 1) * BLK]
            send(12 + t * 2 + part, 6 + part, t)
        mixed = nt(low_h, wo[t]).astype(bf16)
        for j in range(3):
            cols = slice(j * 2 * HD, (j + 1) * 2 * HD)
            q, k, v = qkv_ref[0, t, :, cols], qkv_ref[0, 2 + t, :, cols], qkv_ref[0, 4 + t, :, cols]
            mix = mixed[:, cols]
            dq = dk = dv = jnp.zeros((F, 2 * HD), f32)
            for m in (m0, m1):
                qm, km, gm = q * m, k * m, mix * m
                p = softmax_rows(nt(qm, k) * 0.125)
                dv = dv + tn(p.astype(bf16), gm)
                dp = nt(gm, v)
                ds = (p * (dp - jnp.sum(dp * p, axis=-1, keepdims=True))).astype(bf16)
                dq = dq + nn(ds, km)
                dk = dk + tn(ds, qm)
            dqkv[0, :, cols] = (dq * 0.125).astype(bf16)
            dqkv[1, :, cols] = (dk * 0.125).astype(bf16)
            dqkv[2, :, cols] = dv.astype(bf16)
        for w in range(3):
            grad_w = dqkv[w]
            weight = tn(a_low, grad_w).astype(bf16)
            for part in range(2):
                stage[(w * 2 + t) * 2 + part] = weight[part * BLK : (part + 1) * BLK, :]
                send((w * 2 + t) * 2 + part, w * 2 + part, t)
            acc[...] += nt(grad_w, wq[w * 2 + t])
        return carry

    lax.fori_loop(0, 2, half, 0)
    grad = acc[...]
    vg_ref[0, 0:1, :] = jnp.sum(grad * hat1, axis=0, keepdims=True)
    vg_ref[0, 1:2, :] = jnp.sum(grad, axis=0, keepdims=True)
    grad_x = dxs[...] + norm_back(grad, hat1, spread1, vec_ref[0, 0:1, :])
    dxs[...] = grad_x
    out_ref[...] = grad_x
    for k in range(48):
        grad_copy(k, 0).wait()

    @pl.when(step == LAYERS - 1)
    def _():
        for i in range(4):
            head_copy(i).wait()

        def done(s, carry):
            @pl.when(used[s] == 0)
            def _():
                zero_copy(s, 0).wait()
                zero_copy(s, 1).wait()

            return carry

        lax.fori_loop(0, half_slots, done, 0)


def backward(tab, used, grad_x, vecs, saved, head_grad, slots):
    slot_total = slots.shape[0]
    whole = lambda *s: pl.BlockSpec(s, lambda i, tab, used: (0,) * len(s))
    per = lambda *s: pl.BlockSpec(
        (1,) + s, lambda i, tab, used: (LAYERS - 1 - i,) + (0,) * len(s)
    )
    return pl.pallas_call(
        functools.partial(back_kernel, slot_total),
        out_shape=[
            jax.ShapeDtypeStruct((F, D), f32),
            jax.ShapeDtypeStruct(slots.shape, bf16),
            jax.ShapeDtypeStruct((LAYERS, 8, D), f32),
        ],
        grid_spec=pltpu.PrefetchScalarGridSpec(
            num_scalar_prefetch=2,
            grid=(LAYERS,),
            in_specs=[
                whole(F, D),
                per(8, D),
                per(F, D),
                per(6, F, BLK),
                per(2, F, BLK),
                per(F, D),
                per(8, F, BLK),
                whole(4, BLK, BLK),
                ANY,
            ],
            out_specs=[whole(F, D), ANY, per(8, D)],
            scratch_shapes=[
                pltpu.VMEM((F, D), f32),
                pltpu.VMEM((F, D), f32),
                pltpu.VMEM((48, BLK, BLK), bf16),
                pltpu.VMEM((BLK, BLK), bf16),
                pltpu.VMEM((3, F, BLK), bf16),
            ]
            + [pltpu.VMEM(s, d) for s, d in WEIGHTS]
            + [
                pltpu.SemaphoreType.DMA((48,)),
                pltpu.SemaphoreType.DMA((48,)),
                pltpu.SemaphoreType.DMA((4,)),
                pltpu.SemaphoreType.DMA((slot_total // 2, 2)),
            ],
        ),
        compiler_params=pltpu.CompilerParams(
            dimension_semantics=("arbitrary",), vmem_limit_bytes=VLIM
        ),
    )(tab, used, grad_x, vecs, *saved, head_grad, slots)


MESH = pl.DeviceIdType.MESH
ZS = 4
SPLIT = (336, 560, 640)
ORDERS = ("xyz", "zxy", "zyx", "zxy")


def place():
    dp, t = lax.axis_index("dp"), lax.axis_index("tensor")
    return lax.div(dp, 4), lax.rem(lax.div(dp, 2), 2), lax.rem(dp, 2), t


def device(z, x, c, t):
    return {"dp": (z * 2 + x) * 2 + c, "tensor": t}


def greet(z, x, c, t):
    bar = pltpu.get_barrier_semaphore()

    def hello(*at):
        pl.semaphore_signal(bar, inc=1, device_id=device(*at), device_id_type=MESH)

    hello(z, x, 1 - c, t)
    hello(z, 1 - x, c, t)
    hello(z, x, c, 1 - t)

    @pl.when(z > 0)
    def _():
        hello(z - 1, x, c, t)

    @pl.when(z < ZS - 1)
    def _():
        hello(z + 1, x, c, t)

    inner = jnp.where(z > 0, 1, 0) + jnp.where(z < ZS - 1, 1, 0)
    pl.semaphore_wait(bar, 3 + inner)


def piece_order():
    pieces = []
    for cls in (3, 1, 2, 0):
        for dz in range(1 - ZS, ZS):
            for dx in range(2):
                for dt in range(2):
                    pieces.append((abs(dz) + dx + dt, cls, dz, dx, dt))
    rank = {3: 0, 1: 1, 2: 2, 0: 3}
    pieces.sort(key=lambda p: (p[0], rank[p[1]], abs(p[2])))
    return pieces


def gather_kernel(x_ref, d_ref, out_ref, dout_ref, ssem, rsem, csem, crsem, lsem):
    z, x, c, t = place()
    starts = (0, SPLIT[0], SPLIT[0] + SPLIT[1])

    def rows(cls):
        return pl.ds(starts[cls], SPLIT[cls])

    def spot(cls, zo, xo, co, to):
        if cls == 3:
            return dout_ref.at[zo, xo, co, to]
        return out_ref.at[zo, xo, co, to, rows(cls), :]

    own = pltpu.make_async_copy(x_ref, out_ref.at[z, x, c, t], lsem.at[0])
    own.start()
    down = pltpu.make_async_copy(d_ref, dout_ref.at[z, x, c, t], lsem.at[1])
    down.start()
    greet(z, x, c, t)
    sent = []

    def flat(zo, xo, to):
        return (zo * 2 + xo) * 2 + to

    def push(cond, kind, cls, src, at, target):
        zo, xo, to = at
        f = flat(zo, xo, to)
        core = kind == "c"
        send = csem.at[cls, f] if core else ssem.at["xyrl".index(kind), cls, f]
        recv = crsem.at[cls, f] if core else rsem.at[cls, f]
        copy = pltpu.make_async_remote_copy(
            src_ref=src,
            dst_ref=spot(cls, zo, xo, c, to),
            send_sem=send,
            recv_sem=recv,
            device_id=device(*target),
            device_id_type=MESH,
        )
        sent.append((cond, copy))

        def go():
            copy.start()

        if cond is None:
            go()
        else:
            pl.when(cond)(go)

    def both(a, b):
        return b if a is None else a & b

    for _, cls, dz, dx, dt in piece_order():
        order = ORDERS[cls]
        zo, xo, to = z + dz, lax.rem(x + dx, 2), lax.rem(t + dt, 2)
        off = {"z": dz, "x": dx, "y": dt}
        last = max([i for i in range(3) if off[order[i]] != 0], default=-1)
        valid = None if dz == 0 else ((zo >= 0) & (zo < ZS))
        at = (zo, xo, to)
        if last < 0:
            if cls == 3:
                src = d_ref
            else:
                src = x_ref.at[rows(cls), :]
        else:
            src = spot(cls, zo, xo, c, to)

            def arrived(cls=cls, at=at, src=src):
                pltpu.make_async_remote_copy(
                    src_ref=src,
                    dst_ref=src,
                    send_sem=csem.at[cls, 0],
                    recv_sem=rsem.at[cls, flat(*at)],
                    device_id=device(z, x, 1 - c, t),
                    device_id_type=MESH,
                ).wait_recv()

            if valid is None:
                arrived()
            else:
                pl.when(valid)(arrived)
        right = z < ZS - 1
        left = z > 0
        if last >= 0 and order[last] == "z":
            if dz < 0:
                push(both(valid, right), "r", cls, src, at, (z + 1, x, c, t))
            else:
                push(both(valid, left), "l", cls, src, at, (z - 1, x, c, t))
        for i in range(last + 1, 3):
            if order[i] == "z":
                push(both(valid, right), "r", cls, src, at, (z + 1, x, c, t))
                push(both(valid, left), "l", cls, src, at, (z - 1, x, c, t))
            elif order[i] == "x":
                push(valid, "x", cls, src, at, (z, 1 - x, c, t))
            else:
                push(valid, "y", cls, src, at, (z, x, c, 1 - t))
        push(valid, "c", cls, src, at, (z, x, 1 - c, t))

    own.wait()
    down.wait()
    for cond, copy in sent:
        if cond is None:
            copy.wait_send()
        else:
            pl.when(cond)(copy.wait_send)
    for cls in range(4):
        for zo in range(ZS):
            for xo in range(2):
                for to in range(2):
                    ref = spot(cls, zo, xo, 1 - c, to)
                    pltpu.make_async_remote_copy(
                        src_ref=ref,
                        dst_ref=ref,
                        send_sem=csem.at[cls, 0],
                        recv_sem=crsem.at[cls, flat(zo, xo, to)],
                        device_id=device(z, x, 1 - c, t),
                        device_id_type=MESH,
                    ).wait_recv()


def ring_gather(flat_slots, cols):
    rows, width = flat_slots.shape
    return pl.pallas_call(
        gather_kernel,
        out_shape=[
            jax.ShapeDtypeStruct((ZS, 2, 2, 2, rows, width), bf16),
            jax.ShapeDtypeStruct((ZS, 2, 2, 2) + cols.shape, bf16),
        ],
        in_specs=[pl.BlockSpec(memory_space=pltpu.VMEM)] * 2,
        out_specs=[pl.BlockSpec(memory_space=pl.ANY)] * 2,
        scratch_shapes=[
            pltpu.SemaphoreType.DMA((4, 4, 16)),
            pltpu.SemaphoreType.DMA((4, 16)),
            pltpu.SemaphoreType.DMA((4, 16)),
            pltpu.SemaphoreType.DMA((4, 16)),
            pltpu.SemaphoreType.DMA((2,)),
        ],
        compiler_params=pltpu.CompilerParams(collective_id=0, has_side_effects=True),
    )(flat_slots, cols)

RING = 4
PIECE = ((336, 384), (560, 384), (640, 384), (24, 1664))
CHUNK = (112, 112, 128, 24)


def coord(dim, at):
    return at["zxy".index(dim)]


def free_index(cls, dim, at):
    order = ORDERS[cls]
    idx = 0
    for d in order[: order.index(dim)]:
        idx = idx * (ZS if d == "z" else 2) + coord(d, at)
    return idx


def free_size(cls, dim):
    order = ORDERS[cls]
    n = 1
    for d in order[: order.index(dim)]:
        n *= ZS if d == "z" else 2
    return n


def scatter_kernel(g_ref, dg_ref, out_ref, dout_ref, acc, dacc, *rest):
    bufs = [rest[3 * i : 3 * i + 3] for i in range(4)]
    ring, dring = rest[12:14]
    csem, crsem, ssem, osem = rest[14:18]
    rsems = [rest[18 + 3 * i : 21 + 3 * i] for i in range(4)]
    z, x, c, t = place()
    starts = (0, SPLIT[0], SPLIT[0] + SPLIT[1])

    def rows(cls):
        return pl.ds(starts[cls], SPLIT[cls])

    def flat(at):
        return (at[0] * 2 + at[1]) * 2 + at[2]

    def mine(cls, at, co):
        if cls == 3:
            return dg_ref.at[at[0], at[1], co, at[2]]
        return g_ref.at[at[0], at[1], co, at[2], rows(cls), :]

    def held(cls, f):
        if cls == 3:
            return dacc.at[f]
        return acc.at[f, rows(cls), :]

    plan = []
    for _, cls, dz, dx, dt in reversed(piece_order()):
        zo, xo, to = z + dz, lax.rem(x + dx, 2), lax.rem(t + dt, 2)
        valid = None if dz == 0 else ((zo >= 0) & (zo < ZS))
        plan.append((cls, dz, dx, dt, (zo, xo, to), valid))

    def guard(cond, fn):
        if cond is None:
            fn()
        else:
            pl.when(cond)(fn)

    def own_copy(i):
        cls, _, _, _, at, _ = plan[i]
        if cls == 3:
            dst = dring.at[i % RING]
        else:
            dst = ring.at[i % RING, pl.ds(0, SPLIT[cls]), :]
        return pltpu.make_async_copy(mine(cls, at, c), dst, osem.at[i % RING]), dst

    greet(z, x, c, t)
    core_copies = []
    for i, (cls, dz, dx, dt, at, valid) in enumerate(plan):
        f = flat(at)
        copy = pltpu.make_async_remote_copy(
            src_ref=mine(cls, at, 1 - c),
            dst_ref=held(cls, f),
            send_sem=csem.at[cls, f],
            recv_sem=crsem.at[cls, f],
            device_id=device(z, x, 1 - c, t),
            device_id_type=MESH,
        )
        core_copies.append(copy)
        guard(valid, copy.start)
    for i in range(RING):
        guard(plan[i][5], own_copy(i)[0].start)

    sent = []
    for i, (cls, dz, dx, dt, at, valid) in enumerate(plan):
        order = ORDERS[cls]
        off = {"z": dz, "x": dx, "y": dt}
        last = max([k for k in range(3) if off[order[k]] != 0], default=-1)
        f = flat(at)
        fixed = []
        choice = []

        def slot(dim, idx, cls=cls):
            k = "zxy".index(dim)
            return bufs[cls][k].at[idx], rsems[cls][k].at[idx]

        if last >= 0 and order[last] == "z":
            idx = free_index(cls, "z", at) * (ZS + 1) + at[0]
            choice.append((z < ZS - 1 if dz < 0 else z > 0, slot("z", idx)))
        for k in range(last + 1, 3):
            dim = order[k]
            if dim == "z":
                base = free_index(cls, "z", at) * (ZS + 1)
                choice.append((z < ZS - 1, slot("z", base + z)))
                choice.append((z > 0, slot("z", base + ZS)))
            else:
                fixed.append(slot(dim, free_index(cls, dim, at)))

        dst = held(cls, f)
        copy, own = own_copy(i)

        def arrive(ref, sem):
            pltpu.make_async_remote_copy(
                src_ref=ref,
                dst_ref=ref,
                send_sem=csem.at[0, 0],
                recv_sem=sem,
                device_id=device(z, x, 1 - c, t),
                device_id_type=MESH,
            ).wait_recv()

        def work(i=i, cls=cls, f=f, dst=dst, own=own, copy=copy, fixed=fixed, choice=choice, last=last):
            copy.wait()
            core_copies[i].wait_recv()
            for ref, sem in fixed:
                arrive(ref, sem)
            size, chunk = PIECE[cls][0], CHUNK[cls]

            def add_up(extra):
                refs = [dst, own] + [r for r, _ in fixed] + extra

                def body(k, carry):
                    at_rows = pl.ds(pl.multiple_of(k * chunk, chunk), chunk)
                    total = refs[0][at_rows, :].astype(f32)
                    for r in refs[1:]:
                        total = total + r[at_rows, :].astype(f32)
                    if last < 0:
                        if cls == 3:
                            dout_ref[at_rows, :] = total
                        else:
                            out_ref[pl.ds(starts[cls] + k * chunk, chunk), :] = total
                    else:
                        dst[at_rows, :] = total.astype(bf16)
                    return carry

                lax.fori_loop(0, size // chunk, body, 0)

            if not choice:
                add_up([])
            elif len(choice) == 1:
                cond, (ref, sem) = choice[0]

                @pl.when(cond)
                def _():
                    arrive(ref, sem)
                    add_up([ref])

                @pl.when(jnp.logical_not(cond))
                def _():
                    add_up([])

            else:
                (c0, (r0, s0)), (c1, (r1, s1)) = choice
                n0, n1 = jnp.logical_not(c0), jnp.logical_not(c1)

                @pl.when(c0 & c1)
                def _():
                    arrive(r0, s0)
                    arrive(r1, s1)
                    add_up([r0, r1])

                @pl.when(c0 & n1)
                def _():
                    arrive(r0, s0)
                    add_up([r0])

                @pl.when(n0 & c1)
                def _():
                    arrive(r1, s1)
                    add_up([r1])

        guard(valid, work)
        if i + RING < len(plan):
            guard(plan[i + RING][5], own_copy(i + RING)[0].start)
        if last >= 0:
            dim = order[last]
            zo = at[0]
            if dim == "z":
                base = free_index(cls, "z", at) * (ZS + 1)
                if dz < 0:
                    target, idx = (z - 1, x, c, t), base + zo
                else:
                    target, idx = (z + 1, x, c, t), base + jnp.where(zo == z + 1, ZS, zo)
            else:
                target = (z, 1 - x, c, t) if dim == "x" else (z, x, c, 1 - t)
                idx = free_index(cls, dim, at)
            ref, sem = slot(dim, idx)
            out = pltpu.make_async_remote_copy(
                src_ref=dst,
                dst_ref=ref,
                send_sem=ssem.at[cls, f],
                recv_sem=sem,
                device_id=device(*target),
                device_id_type=MESH,
            )
            guard(valid, out.start)
            sent.append((valid, out))
    for valid, out in sent:
        guard(valid, out.wait_send)
    for i, (_, _, _, _, _, valid) in enumerate(plan):
        guard(valid, core_copies[i].wait_send)


def ring_scatter(g, dg):
    rows, width = g.shape[-2:]
    scratch = [pltpu.VMEM((16, rows, width), bf16), pltpu.VMEM((16,) + dg.shape[-2:], bf16)]
    sems = []
    for cls in range(4):
        for dim in "zxy":
            n = free_size(cls, dim) * (ZS + 1 if dim == "z" else 1)
            scratch.append(pltpu.VMEM((n,) + PIECE[cls], bf16))
            sems.append(pltpu.SemaphoreType.DMA((n,)))
    scratch += [pltpu.VMEM((RING, 640, width), bf16), pltpu.VMEM((RING, 24, 1664), bf16)]
    scratch += [pltpu.SemaphoreType.DMA((4, 16))] * 3 + [pltpu.SemaphoreType.DMA((RING,))]
    return pl.pallas_call(
        scatter_kernel,
        out_shape=[
            jax.ShapeDtypeStruct((rows, width), f32),
            jax.ShapeDtypeStruct(dg.shape[-2:], f32),
        ],
        in_specs=[pl.BlockSpec(memory_space=pl.ANY)] * 2,
        out_specs=[pl.BlockSpec(memory_space=pltpu.VMEM)] * 2,
        scratch_shapes=scratch + sems,
        compiler_params=pltpu.CompilerParams(
            collective_id=1, has_side_effects=True, vmem_limit_bytes=62 * 2**20
        ),
    )(g, dg)


def finish_kernel(red_ref, dred_ref, loss_ref, out_ref, full_ref, cur, got, gz, ssem, rsem, dsem):
    z, x, c, t = place()
    bar = pltpu.get_barrier_semaphore()
    near = [(z, x, 1 - c, t), (z, 1 - x, c, t), (z, x, c, 1 - t)]
    far = [(lax.rem(z + k, ZS), x, c, t) for k in range(1, ZS)]
    for target in near + far:
        pl.semaphore_signal(bar, inc=1, device_id=device(*target), device_id_type=MESH)
    pl.semaphore_wait(bar, len(near) + len(far))
    half = dred_ref.shape[0]
    at = pl.ds(pl.multiple_of(t * half, half), half)
    swap = pltpu.make_async_remote_copy(
        src_ref=dred_ref,
        dst_ref=full_ref.at[at, :],
        send_sem=dsem.at[0],
        recv_sem=dsem.at[1],
        device_id=device(z, x, c, 1 - t),
        device_id_type=MESH,
    )
    swap.start()
    full_ref[at, :] = dred_ref[...]

    def square(k, total):
        v = red_ref[pl.ds(pl.multiple_of(k * 96, 96), 96), :]
        return total + jnp.sum((v * v).reshape(12, 8, width), axis=0)

    width = red_ref.shape[1]
    total = lax.fori_loop(0, red_ref.shape[0] // 96, square, jnp.zeros((8, width), f32))
    d = dred_ref[...]
    extra = jnp.sum((d * d).reshape(half // 8, 8, d.shape[1]), axis=0)
    norm = jnp.sum(total, axis=1, keepdims=True) + jnp.sum(extra, axis=1, keepdims=True)
    norm = jnp.sum(norm, axis=0, keepdims=True)
    row = lax.broadcasted_iota(jnp.int32, (8, 128), 0)
    cur[0] = jnp.where(row == 0, loss_ref[...], jnp.broadcast_to(norm, (8, 128)))
    for k, target in enumerate(near):
        copy = pltpu.make_async_remote_copy(
            src_ref=cur.at[k],
            dst_ref=got.at[k],
            send_sem=ssem.at[k],
            recv_sem=rsem.at[k],
            device_id=device(*target),
            device_id_type=MESH,
        )
        copy.start()
        copy.wait()
        cur[k + 1] = cur[k] + got[k]
    gz[z] = cur[3]
    copies = []
    for k, target in enumerate(far):
        copy = pltpu.make_async_remote_copy(
            src_ref=cur.at[3],
            dst_ref=gz.at[z],
            send_sem=ssem.at[3 + k],
            recv_sem=rsem.at[3 + k],
            device_id=device(*target),
            device_id_type=MESH,
        )
        copy.start()
        copies.append(copy)
    for copy in copies:
        copy.wait()
    out_ref[...] = (gz[0] + gz[1]) + (gz[2] + gz[3])
    swap.wait()


def ring_finish(red, dred, loss_tile):
    vm = pl.BlockSpec(memory_space=pltpu.VMEM)
    return pl.pallas_call(
        finish_kernel,
        out_shape=[
            jax.ShapeDtypeStruct((8, 128), f32),
            jax.ShapeDtypeStruct((2 * dred.shape[0], dred.shape[1]), f32),
        ],
        in_specs=[vm] * 3,
        out_specs=[vm] * 2,
        scratch_shapes=[
            pltpu.VMEM((4, 8, 128), f32),
            pltpu.VMEM((3, 8, 128), f32),
            pltpu.VMEM((ZS, 8, 128), f32),
            pltpu.SemaphoreType.DMA((6,)),
            pltpu.SemaphoreType.DMA((6,)),
            pltpu.SemaphoreType.DMA((2,)),
        ],
        compiler_params=pltpu.CompilerParams(collective_id=2, has_side_effects=True),
    )(red, dred, loss_tile)


def span_mask(mask_starts, frames):
    positions = jnp.arange(frames, dtype=jnp.int32)[None, :, None]
    starts = mask_starts[:, None, :]
    inside = (positions >= starts) & (positions < starts + MASK_LEN)
    return jnp.any(inside, axis=-1).astype(f32)


def widen(cols, digits):
    rows = cols.shape[0]
    end = C + CONV
    return jnp.concatenate(
        [
            cols[:, :end],
            jnp.zeros((rows, VEC_AT - end), cols.dtype),
            cols[:, end:],
            jnp.zeros((rows, COUNT_AT - NVEC), cols.dtype),
            jnp.broadcast_to(digits.astype(cols.dtype)[None, :], (rows, 2)),
            jnp.zeros((rows, WIDE - VEC_AT - COUNT_AT - 2), cols.dtype),
        ],
        axis=1,
    )


def narrow(cols):
    return jnp.concatenate([cols[:, : C + CONV], cols[:, VEC_AT : VEC_AT + NVEC]], axis=1)


def vectors_of(dense_low):
    rows = dense_low[:, VEC_AT : VEC_AT + 16].T.astype(f32)
    per_layer = rows[1 : 1 + 4 * LAYERS].reshape(LAYERS, 4, D)
    per_layer = jnp.pad(per_layer, ((0, 0), (0, 4), (0, 0)))
    final = jnp.pad(rows[1 + 4 * LAYERS : 3 + 4 * LAYERS], ((0, 6), (0, 0)))
    return per_layer, final


def gather_params(local_slots, cols, digits):
    low = local_slots[:, 0].astype(bf16)
    wide = widen(cols.astype(bf16), digits)
    if not ringed():
        slots = lax.all_gather(low, ("dp", "tensor"), axis=0, tiled=True)
        return slots, lax.all_gather(wide, "dp", axis=0, tiled=True)
    half = wide.shape[0] // 2
    part = lax.dynamic_slice_in_dim(wide, lax.axis_index("tensor") * half, half, axis=0)
    slots, dense = ring_gather(low.reshape(-1, BLK), part)
    return slots.reshape(-1, BLK, BLK), dense.reshape(-1, WIDE)


def ringed():
    return lax.axis_size("dp") == 4 * ZS and lax.axis_size("tensor") == 2


def reduce_grads(slot_part, col_part, loss_tile):
    if not ringed():
        slot_sum = lax.psum_scatter(slot_part, ("dp", "tensor"), scatter_dimension=0, tiled=True)
        col_sum = lax.psum_scatter(col_part.astype(f32), "dp", scatter_dimension=0, tiled=True)
        col_sum = lax.psum(col_sum, "tensor")
        reduced = slot_sum.astype(f32)
        square = jnp.sum(reduced * reduced) + 0.5 * jnp.sum(col_sum * col_sum)
        loss_value, square_sum = lax.psum((loss_tile[0, 0], square), ("dp", "tensor"))
        return reduced, col_sum, loss_value, square_sum
    shape = (ZS, 2, 2, 2)
    slots = slot_part.reshape(shape + (-1, BLK))
    slot_sum, col_sum = ring_scatter(slots, col_part.reshape(shape + (-1, WIDE)))
    tile, cols = ring_finish(slot_sum, col_sum, loss_tile)
    return slot_sum.reshape(-1, BLK, BLK), cols, tile[0, 0], tile[1, 0]


def local(
    features,
    mask_starts,
    block_slot,
    settings,
    matrices,
    momentum,
    statistics,
    inverse_roots,
    teacher,
    dense_params,
    dense_moment,
    dense_second,
    teacher_dense,
):
    held = matrices.shape[0]
    dp = lax.axis_size("dp")
    slot_total = held * dp
    half = lax.axis_index("tensor")
    masked_all = span_mask(mask_starts, F)
    count = jnp.sum(masked_all)
    high = jnp.floor(count / COUNT_BASE)
    digits = jnp.stack([high, count - COUNT_BASE * high])
    feat = lax.dynamic_index_in_dim(features, half, axis=0, keepdims=False)
    masked = lax.dynamic_index_in_dim(masked_all, half, axis=0, keepdims=False)
    mask_row, mask_col = masked[None, :], masked[:, None]

    base = (block_slot // held) * (2 * held) + block_slot % held
    tab = jnp.concatenate([base, base + held]).astype(jnp.int32)
    ids = jnp.arange(slot_total, dtype=jnp.int32)
    taken = jnp.any(block_slot[None, :] == ids[:, None], axis=1).astype(jnp.int32)
    places = (ids // held) * (2 * held) + ids % held
    used = jnp.concatenate([taken, places, jnp.full((8,), held, jnp.int32)]).astype(jnp.int32)

    teach_slots, teach_dense = gather_params(teacher, teacher_dense, digits)
    low_slots, low_dense = gather_params(matrices, dense_params, digits)
    counts = low_dense[:: dense_params.shape[0], VEC_AT + COUNT_AT : VEC_AT + COUNT_AT + 2]
    mask_total = jnp.sum(counts.astype(f32) * jnp.array([COUNT_BASE, 1.0], f32))
    loss_scale = 1.0 / (mask_total * math.sqrt(D))

    teach_vecs, _ = vectors_of(teach_dense)
    teach_x = front(teach_dense, feat, mask_row, False)
    (target,) = encoder(tab, teach_x, teach_vecs, teach_slots, False)

    vecs, final_vec = vectors_of(low_dense)
    x0, emb, conv_out = front(low_dense, feat, mask_row, True)
    x_last, *saved = encoder(tab, x0, vecs, low_slots, True)
    grad_x, head_grad, head_vg, loss_tile = head(
        tab, x_last, final_vec, target, mask_col, loss_scale.reshape(1, 1), low_slots
    )
    grad_x, slot_part, layer_vg = backward(
        tab, used, grad_x, vecs, saved, head_grad, low_slots
    )
    vec_rows = jnp.concatenate(
        [
            jnp.zeros((1, D), f32),
            layer_vg[:, :4].reshape(4 * LAYERS, D),
            head_vg[:2],
            jnp.zeros((128 - NVEC, D), f32),
        ],
        axis=0,
    )
    col_part = front_back(low_dense, feat, mask_row, grad_x, emb, conv_out, vec_rows)

    reduced, cols, loss_value, square_sum = reduce_grads(slot_part, col_part, loss_tile)
    reduced_cols = narrow(cols)
    grad_norm = jnp.sqrt(square_sum)
    factor = jnp.minimum(1.0, settings[1] / grad_norm)
    squared = factor * factor
    low = reduced.astype(bf16)
    left_new = state_decay * statistics[:, 0, 0] + ((1.0 - state_decay) * squared) * jnp.einsum(
        "sij,skj->sik", low, low, preferred_element_type=f32
    )
    right_new = state_decay * statistics[:, 0, 1] + ((1.0 - state_decay) * squared) * jnp.einsum(
        "sji,sjk->sik", low, low, preferred_element_type=f32
    )
    left_side = jnp.einsum(
        "sij,sjk->sik", inverse_roots[:, 0, 0], reduced, precision=lax.Precision.HIGH
    )
    precond = jnp.einsum(
        "sij,sjk->sik", left_side, inverse_roots[:, 0, 1], precision=lax.Precision.HIGH
    )
    momentum_new = state_decay * momentum[:, 0] + ((1.0 - state_decay) * factor) * precond
    matrices_new = matrices[:, 0] - matrix_rate * momentum_new
    teacher_new = settings[0] * teacher[:, 0] + (1.0 - settings[0]) * matrices_new
    statistics_new = jnp.stack([left_new, right_new], axis=1)[:, None]
    grad_small = reduced_cols * factor
    dense_moment_new = state_decay * dense_moment + (1.0 - state_decay) * grad_small
    dense_second_new = state_decay * dense_second + (1.0 - state_decay) * grad_small * grad_small
    dense_new = dense_params - dense_rate * dense_moment_new / (
        jnp.sqrt(dense_second_new) + adam_eps
    )
    teacher_dense_new = settings[0] * teacher_dense + (1.0 - settings[0]) * dense_new
    return (
        loss_value,
        grad_norm,
        matrices_new[:, None],
        momentum_new[:, None],
        statistics_new,
        teacher_new[:, None],
        dense_new,
        dense_moment_new,
        dense_second_new,
        teacher_dense_new,
    )


def solution(mesh):
    blocks = P("dp", "tensor", None, None)
    pairs = P("dp", "tensor", None, None, None)
    rows = P("dp", None)
    return jax.shard_map(
        local,
        mesh=mesh,
        in_specs=(P("dp", None, None), rows, P(), P(), blocks, blocks, pairs, pairs, blocks)
        + (rows,) * 4,
        out_specs=(P(), P(), blocks, blocks, pairs, blocks) + (rows,) * 4,
        check_vma=False,
    )
```

time: 1780 us -> 724 us (0.41)
  waiting for transfers between devices: 669 us -> 0 us
  Pallas kernels: 0 us -> 661 us
  local copies, waits for them, and re-layouts: 601 us -> 18.2 us
  matrix products: 274 us -> 10.4 us
  other arithmetic: 130 us -> 20.1 us
  blocking collectives: 73.3 us -> 0 us
  between operations: 26.6 us -> 6.56 us
    pallas_call x0 -> x11, Pallas kernels: none -> 661 us  [the longest x2 328 us: ring_gather(): pl.pallas_call(gather_kernel, out_shape=[jax.ShapeDtypeStruct((ZS, 2, 2,...]
    reduce_scatter x2 -> x0, waiting for transfers between devices: 360 us -> none  [the longest x1 360 us: local(): lax.psum_scatter(slot_part, 'dp', scatter_dimension=0, tiled=True)]
    dot_general x259 -> x3, matrix products: 269 us -> 6.15 us  [the longest x1 4.16 us: local(): jnp.einsum('sij,sjk->sik', inverse_roots[:, 0, 0], reduced, precision=lax...]
    all_gather x4 -> x0, waiting for transfers between devices: 157 us -> none  [the longest x1 86.9 us: local(): lax.all_gather(teacher.astype(jnp.bfloat16), 'dp', axis=0, tiled=True)]
    psum x9 -> x0, waiting for transfers between devices: 152 us -> none  [the longest x4 107 us: branch_total(): lax.psum(partial_value.astype(jnp.bfloat16), 'tensor').astype(jnp.float32)]
    unnamed x1033 -> x30, local copies, waits for them, and re-layouts: 133 us -> 4.29 us
    reshape x46 -> x4, local copies, waits for them, and re-layouts: 113 us -> 0.85 us  [the longest x1 0.8 us: reduce_grads(): return (slot_sum.reshape(-1, BLK, BLK), cols, tile[0, 0], tile[1, 0])]
    scatter x2 -> x0, local copies, waits for them, and re-layouts: 103 us -> none  [owner_layout(): jnp.zeros((slot_total, 1) + blocks.shape[1:], jnp.float32).at[block_slot, 0]]
  transfers between devices with their start and end apart: 15 -> 0, of which waited for: 13 -> 0; matrix products, arithmetic and copies ran while one was open for 28% -> 0% of each run, Pallas kernels for 0% -> 0%
where the time goes in v1:
time: 724 us; the launch traced here: 716 us
  Pallas kernels  661 us (91%)
  other arithmetic  20.1 us (3%)
  local copies, waits for them, and re-layouts  18.2 us (3%)
  matrix products  10.4 us (1%)
    pallas_call x2, Pallas kernels, ring_gather(): pl.pallas_call(gather_kernel, out_shape=[jax.ShapeDtypeStruct((ZS, 2, 2,...  328 us
    pallas_call x1, Pallas kernels, ring_scatter(): pl.pallas_call(scatter_kernel, out_shape=[jax.ShapeDtypeStruct((rows, wid...  153 us
    pallas_call x1, Pallas kernels, backward(): pl.pallas_call(functools.partial(back_kernel, slot_total), out_shape=[jax...  57.8 us
    pallas_call x2, Pallas kernels, encoder(): pl.pallas_call(functools.partial(encoder_kernel, keep), out_shape=outs, g...  54.9 us
    pallas_call x1, Pallas kernels, ring_finish(): pl.pallas_call(finish_kernel, out_shape=[jax.ShapeDtypeStruct((8, 128), f...  26.8 us
    pallas_call x2, Pallas kernels, front(): pl.pallas_call(functools.partial(front_kernel, keep), out_shape=outs, in_...  17.5 us
    pallas_call x1, Pallas kernels, front_back(): pl.pallas_call(front_back_kernel, out_shape=jax.ShapeDtypeStruct((D, WIDE...  16.3 us

profile of v1, /device:TPU:0, one launch (start us, length us, event | category | flops | bytes accessed | tf_op | source)
XLA Modules:
  0.0 715.8 jit_solution(7768722118852059848)
XLA Ops:
  0.6 0.0 copy-start
  0.7 0.8 fusion.21
  1.5 0.1 pad.24.clone
  1.6 0.7 pad_add_fusion.used
  2.3 0.7 broadcast_add_fusion
  2.9 0.8 fusion.20
  3.7 0.6 convert_reduce_fusion
  5.6 0.1 pad_maximum_fusion
  5.7 0.6 constant_dynamic-slice_fusion.1.mask_ref
  6.3 1.3 fusion.28
  8.3 0.7 broadcast_add_fusion.1
  8.9 0.6 pad_add_fusion.1.tab
  9.5 0.8 copy.60.mask_ref
  10.3 1.0 convert_element_type.56
  11.3 0.1 slice.93
  11.4 0.1 concatenate.25
  11.5 1.0 convert_element_type.62
  12.5 0.1 slice.98
  12.6 0.1 concatenate.26
  12.7 0.7 constant_dynamic-slice_fusion
  13.4 0.7 dynamic-slice_bitcast_fusion.feat_ref
  14.1 2.8 convert_element_type.54
  16.9 1.1 convert_element_type.60
  18.1 165.5 %shard_map.216 = (bf16[4,2,2,2,1536,384]{5,4,3,2,1,0:T(8,128)(2,1)}, bf16[4,2,2,2,24,1664]{5,4,3,2,1,0:T(8,128)(2,1)}) custom-call(bf16[1536,384]{1,0:T(8,128)(2,1)} %bitcast.126, bf16[24,1664]{1,0:T(8,128)(2,1)} %get-tuple-element.100.d_ref), custom_call_target="tpu_custom_call" | custom-call | tf_op jit(solution)/shard_map/pallas_call | solution.py:831
  183.6 0.9 slice_bitcast_fusion
  184.5 8.7 %shard_map.217.x_ref = f32[256,768]{1,0:T(8,128)} custom-call(bf16[768,1664]{1,0:T(8,128)(2,1)} %bitcast.128, bf16[256,512]{1,0:T(8,128)(2,1)} %dynamic-slice_bitcast_fusion.feat_ref, f32[1,256]{1,0:T(1,128)} %constant_dynamic-slice_fusion.1.mask_ref), custom_call_target="tpu_custom_call" | custom-call | tf_op jit(solution)/shard_map/pallas_call | solution.py:144
  193.3 0.1 slice.100
  193.4 0.1 copy.58
  193.5 0.6 pad_convert_fusion.vec_ref
  194.2 26.6 %shard_map.218.target_ref = f32[256,768]{1,0:T(8,128)} custom-call(s32[100]{0:T(128)} %pad_add_fusion.1.tab, f32[256,768]{1,0:T(8,128)} %shard_map.217.x_ref, f32[2,8,768]{2,1,0:T(8,128)} %pad_convert_fusion.vec_ref, bf16[128,384,384]{2,1,0:T(8,128)(2,1)} %bitcast.114), custom_call_target="tpu_custom_call" | custom-call | tf_op jit(solution)/shard_map/pallas_call | solution.py:370
  220.8 162.9 %shard_map.213 = (bf16[4,2,2,2,1536,384]{5,4,3,2,1,0:T(8,128)(2,1)}, bf16[4,2,2,2,24,1664]{5,4,3,2,1,0:T(8,128)(2,1)}) custom-call(bf16[1536,384]{1,0:T(8,128)(2,1)} %bitcast.125, bf16[24,1664]{1,0:T(8,128)(2,1)} %get-tuple-element.101.d_ref), custom_call_target="tpu_custom_call" | custom-call | tf_op jit(solution)/shard_map/pallas_call | solution.py:831
  383.7 1.0 slice.79
  384.8 0.6 multiply_reduce_fusion
  386.0 1.0 convert_bitcast_fusion
  387.0 0.2 slice.96
  387.2 0.2 copy.86
  387.3 0.2 slice.95
  387.5 0.1 copy.57
  387.7 0.6 pad.14.clone.vec_ref
  388.3 0.6 pad.13.vec_ref
  388.9 8.7 %shard_map.214 = (f32[256,768]{1,0:T(8,128)}, f32[768,256]{1,0:T(8,128)}, f32[768,256]{1,0:T(8,128)}) custom-call(bf16[768,1664]{1,0:T(8,128)(2,1)} %bitcast.119, bf16[256,512]{1,0:T(8,128)(2,1)} %dynamic-slice_bitcast_fusion.feat_ref, f32[1,256]{1,0:T(1,128)} %constant_dynamic-slice_fusion.1.mask_ref), custom_call_target="tpu_custom_call" | custom-call | tf_op jit(solution)/shard_map/pallas_call | solution.py:144
  397.6 28.3 %shard_map.215 = (f32[256,768]{1,0:T(8,128)}, f32[2,256,768]{2,1,0:T(8,128)}, bf16[2,6,256,384]{3,2,1,0:T(8,128)(2,1)}, bf16[2,2,256,384]{3,2,1,0:T(8,128)(2,1)}...) custom-call(s32[100]{0:T(128)} %pad_add_fusion.1.tab, f32[256,768]{1,0:T(8,128)} %get-tuple-element.35.x_ref, ...), custom_call_target="tpu_custom_call" | custom-call | tf_op jit(solution)/shard_map/pallas_call | solution.py:370
  426.0 6.2 shard_map.219
  432.2 57.8 %shard_map.220 = (f32[256,768]{1,0:T(8,128)}, bf16[128,384,384]{2,1,0:T(8,128)(2,1)}, f32[2,8,768]{2,1,0:T(8,128)}) custom-call(s32[100]{0:T(128)} %pad_add_fusion.1.tab, s32[136]{0:T(256)} %pad_add_fusion.used, f32[256,768]{1,0:T(8,128)} %get-tuple-element.40.dx_ref, f32[2,8,768]{2,1,0:T(8,128)} %pad.13.vec_ref, f32[2,256,768]{2,1,0:T(8,128)} %get-tuple-element.41.xin_ref, ...), custom_call_target="tpu_custom_call" | custom-call | tf_op jit(solution)/shard_map/pallas_call | solution.py:620
  489.9 0.7 slice.81
  490.7 0.8 slice.80
  491.5 0.8 maximum_maximum_fusion.vec_ref
  492.3 16.3 %shard_map.221 = bf16[768,1664]{1,0:T(8,128)(2,1)} custom-call(bf16[768,1664]{1,0:T(8,128)(2,1)} %bitcast.120, bf16[256,512]{1,0:T(8,128)(2,1)} %dynamic-slice_bitcast_fusion.feat_ref, f32[1,256]{1,0:T(1,128)} %constant_dynamic-slice_fusion.1.mask_ref, f32[256,768]{1,0:T(8,128)} %get-tuple-element.48.dx_ref, f32[768,256]{1,0:T(8,128)} %get-tuple-element.49.emb_ref, ...), custom_call_target="tpu_custom_call" | custom-call | tf_op jit(solution)/shard_map/pallas_call | solution.py:196
  508.7 152.5 %shard_map.222 = (f32[1536,384]{1,0:T(8,128)}, f32[24,1664]{1,0:T(8,128)}) custom-call(bf16[4,2,2,2,1536,384]{5,4,3,2,1,0:T(8,128)(2,1)} %bitcast.113, bf16[4,2,2,2,24,1664]{5,4,3,2,1,0:T(8,128)(2,1)} %bitcast.121), custom_call_target="tpu_custom_call" | custom-call | tf_op jit(solution)/shard_map/pallas_call | solution.py:1076
  661.3 26.8 %shard_map.223 = (f32[8,128]{1,0:T(8,128)}, f32[48,1664]{1,0:T(8,128)}) custom-call(f32[1536,384]{1,0:T(8,128)} %get-tuple-element.53.red_ref, f32[24,1664]{1,0:T(8,128)} %get-tuple-element.54.dred_ref, f32[8,128]{1,0:T(8,128)} %get-tuple-element.55.loss_ref), custom_call_target="tpu_custom_call" | custom-call | tf_op jit(solution)/shard_map/pallas_call | solution.py:1157
  688.1 1.3 fusion.27
  690.7 0.7 slice.91
  691.5 1.0 slice.90
  692.5 2.7 multiply_add_fusion.1
  695.2 0.8 copy.67
  696.0 4.2 fusion.8
  700.2 0.0 slice-start.1
  700.2 4.2 bitcast_add_fusion.1
  704.5 1.0 fusion.2
  705.5 1.0 fusion.5
  706.5 0.3 maximum_bitcast_fusion
  706.9 2.7 copy.75
  709.6 1.3 copy-done.5
  710.9 3.2 fusion.10
  (40 shorter events, 0.2 us)
Async XLA Ops:
  0.6 12.8 %copy-start = (bf16[2,256,512]{2,1,0:T(8,128)(2,1)S(1)}, bf16[2,256,512]{2,1,0:T(8,128)(2,1)}, u32[]{:S(2)}) copy-start(bf16[2,256,512]{2,1,0:T(8,128)(2,1)} %param.14) | copy-start | bytes 1572868
  12.7 4.2 copy-start.4
  194.2 190.6 %copy-start.11 = (f32[2]{0:T(128)S(1)}, f32[2]{0:T(128)}, u32[]{:S(2)}) copy-start(f32[2]{0:T(128)} %constant.102.clone) | copy-start | bytes 28
  661.2 31.2 %copy-start.8 = (f32[48,1435]{1,0:T(8,128)S(1)}, f32[48,1435]{1,0:T(8,128)}, u32[]{:S(2)}) copy-start(f32[48,1435]{1,0:T(8,128)} %param.26) | copy-start | bytes 826564
  661.2 31.2 %copy-start.9 = (f32[48,1435]{1,0:T(8,128)S(1)}, f32[48,1435]{1,0:T(8,128)}, u32[]{:S(2)}) copy-start(f32[48,1435]{1,0:T(8,128)} %param.23) | copy-start | bytes 826564
  661.3 31.2 %copy-start.10 = (f32[48,1435]{1,0:T(8,128)S(1)}, f32[48,1435]{1,0:T(8,128)}, u32[]{:S(2)}) copy-start(f32[48,1435]{1,0:T(8,128)} %param.24) | copy-start | bytes 826564
  661.3 33.9 %copy-start.2 = (f32[1536,384]{1,0:T(8,128)S(1)}, f32[1536,384]{1,0:T(8,128)}, u32[]{:S(2)}) copy-start(f32[1536,384]{1,0:T(8,128)} %get-tuple-element.53.red_ref) | copy-start | bytes 7077892
  696.0 4.2 copy-start.7
  696.0 8.5 %slice-start = ((s8[4718592]{0:T(1024)(128)(4,1)}), s8[4194304]{0:T(1024)(128)(4,1)S(1)}, s32[]{:S(2)}) async-start(s8[4718592]{0:T(1024)(128)(4,1)} %bitcast.123), calls=%async_computation | async-start | bytes 8388608
  700.2 4.3 slice-start.1
  704.5 5.1 copy-start.6
  706.9 2.7 copy-start.3
  706.9 4.1 copy-start.5
  710.9 3.2 copy-start.1

commit v2 on v1

--- a/solution.py
+++ b/solution.py
@@ -16,6 +16,7 @@
 GROUPS = 16
 LAYERS = 2
 MASK_LEN = 10
+SPANS = 16
 BLK = 384
 GW = 48
 F = 256
@@ -27,6 +28,7 @@
 NVEC = 3 + 4 * LAYERS
 MARGIN = KERNEL // 2
 COUNT_AT = 16
+VROWS = 24
 COUNT_BASE = 16.0
 
 norm_eps = 1e-05
@@ -107,17 +109,15 @@
         win_ref[tap * GW : (tap + 1) * GW, :] = moved.astype(bf16)
 
 
-def front_kernel(keep, w_ref, feat_ref, mask_ref, *refs):
+def front_kernel(keep, starts_ref, w_ref, feat_ref, x_ref, vec_ref, emb_ref, conv_ref, low_s, win_s):
+    clip = lax.axis_index("tensor")
+    proj = nt(w_ref[:, :C], feat_ref[clip])
+    vec = w_ref[:, VEC_AT : VEC_AT + 128].astype(f32)
+    vec_ref[...] = vec.T[:VROWS]
     if keep:
-        x_ref, emb_ref, conv_ref, low_s, win_s = refs
-    else:
-        x_ref, emb_ref, conv_ref, low_s, win_s = (refs[0],) + refs[1:]
-    proj = nt(w_ref[:, :C], feat_ref[...])
-    if keep:
-        vec = w_ref[:, VEC_AT : VEC_AT + 128].astype(f32)
         lane = lax.broadcasted_iota(jnp.int32, (1, 128), 1)
         col = jnp.sum(jnp.where(lane == 0, vec, 0.0), axis=1, keepdims=True)
-        proj = jnp.where(mask_ref[...] > 0, col, proj)
+        proj = jnp.where(span_row(starts_ref, clip, 1) > 0, col, proj)
     emb_ref[...] = proj
     low_s[...] = proj.astype(bf16).astype(f32)
     win_s[CONV:, :] = jnp.zeros((CONV_PAD - CONV, F), bf16)
@@ -132,28 +132,42 @@
     x_ref[...] = (emb_ref[...] + gelu(conv_ref[...])).T
 
 
-def front(dense_low, feat, mask_row, keep):
+def front(mask_starts, dense_low, features, keep):
     big = jax.ShapeDtypeStruct((D, F), f32)
     vm = pl.BlockSpec(memory_space=pltpu.VMEM)
     scratch = [pltpu.VMEM((D, F), f32), pltpu.VMEM((CONV_PAD, F), bf16)]
+    outs = [jax.ShapeDtypeStruct((F, D), f32), jax.ShapeDtypeStruct((VROWS, D), f32)]
     if keep:
-        outs, specs = (jax.ShapeDtypeStruct((F, D), f32), big, big), (vm, vm, vm)
+        outs += [big, big]
     else:
-        outs, specs = jax.ShapeDtypeStruct((F, D), f32), vm
         scratch = [pltpu.VMEM((D, F), f32), pltpu.VMEM((D, F), f32)] + scratch
     return pl.pallas_call(
         functools.partial(front_kernel, keep),
         out_shape=outs,
-        in_specs=[vm, vm, vm],
-        out_specs=specs,
+        in_specs=[pl.BlockSpec(memory_space=pltpu.SMEM), vm, vm],
+        out_specs=[vm] * len(outs),
         scratch_shapes=scratch,
         compiler_params=pltpu.CompilerParams(vmem_limit_bytes=VLIM),
-    )(dense_low, feat, mask_row)
+    )(mask_starts, dense_low, features)
 
 
 def front_back_kernel(
-    w_ref, feat_ref, mask_ref, dx_ref, emb_ref, conv_ref, vec_ref, out_ref, low_s, dcv_s, dem_s, win_s
+    starts_ref,
+    w_ref,
+    feat_ref,
+    dx_ref,
+    emb_ref,
+    conv_ref,
+    layer_ref,
+    final_ref,
+    out_ref,
+    low_s,
+    dcv_s,
+    dem_s,
+    win_s,
+    vec_s,
 ):
+    clip = lax.axis_index("tensor")
     grad_x = dx_ref[...].T
     _, slope = gelu_both(conv_ref[...])
     dcv_s[...] = (slope * grad_x).astype(bf16)
@@ -182,30 +196,35 @@
 
     lax.fori_loop(0, GROUPS, group, 0)
     grad_emb = grad_x + dem_s[...]
-    mask = mask_ref[...]
+    mask = span_row(starts_ref, clip, 1)
     mask_grad = jnp.sum(grad_emb * mask, axis=1, keepdims=True)
     grad_proj = (grad_emb * (1.0 - mask)).astype(bf16)
-    out_ref[:, :C] = nn(grad_proj, feat_ref[...]).astype(out_ref.dtype)
-    vec_t = vec_ref[...].T
+    out_ref[:, :C] = nn(grad_proj, feat_ref[clip]).astype(out_ref.dtype)
+    vec_s[...] = jnp.zeros_like(vec_s)
+    for layer in range(LAYERS):
+        vec_s[1 + 4 * layer : 5 + 4 * layer, :] = layer_ref[layer, :4, :]
+    vec_s[1 + 4 * LAYERS : NVEC, :] = final_ref[:2, :]
+    vec_t = vec_s[...].T
     at = lax.broadcasted_iota(jnp.int32, (1, 128), 1)
     out_ref[:, VEC_AT:] = jnp.where(at == 0, mask_grad, vec_t).astype(out_ref.dtype)
 
 
-def front_back(dense_low, feat, mask_row, grad_x, emb, conv_out, vec_grads):
+def front_back(mask_starts, dense_low, features, grad_x, emb, conv_out, layer_vg, final_vg):
     vm = pl.BlockSpec(memory_space=pltpu.VMEM)
     return pl.pallas_call(
         front_back_kernel,
         out_shape=jax.ShapeDtypeStruct((D, WIDE), bf16),
-        in_specs=[vm] * 7,
+        in_specs=[pl.BlockSpec(memory_space=pltpu.SMEM)] + [vm] * 7,
         out_specs=vm,
         scratch_shapes=[
             pltpu.VMEM((D, F), f32),
             pltpu.VMEM((D, F), bf16),
             pltpu.VMEM((D, F), f32),
             pltpu.VMEM((CONV_PAD, F), bf16),
+            pltpu.VMEM((128, D), f32),
         ],
         compiler_params=pltpu.CompilerParams(vmem_limit_bytes=VLIM),
-    )(dense_low, feat, mask_row, grad_x, emb, conv_out, vec_grads)
+    )(mask_starts, dense_low, features, grad_x, emb, conv_out, layer_vg, final_vg)
 
 
 def weight_plan():
@@ -235,9 +254,14 @@
     return ref.at[at, :, pl.ds(part * BLK, BLK)]
 
 
-def start_weights(tab, layer, w_hbm, refs, sem):
+def spot_of(held, slots, t, block):
+    slot = slots[block]
+    return lax.div(slot, held) * (2 * held) + t * held + lax.rem(slot, held)
+
+
+def start_weights(held, slots, layer, w_hbm, refs, sem):
     for k, (t, off, which, at, part) in enumerate(weight_plan()):
-        src = tab[t * NBLK + layer * 24 + off]
+        src = spot_of(held, slots, t, layer * 24 + off)
         pltpu.make_async_copy(w_hbm.at[src], block_view(refs, which, at, part), sem.at[k]).start()
 
 
@@ -264,7 +288,7 @@
 ]
 
 
-def encoder_kernel(keep, tab, x_ref, vec_ref, w_hbm, *refs):
+def encoder_kernel(keep, held, tab, x_ref, vec_ref, w_hbm, *refs):
     if keep:
         out_ref, xin_ref, qkv_ref, o_ref, h_ref, z_ref = refs[:6]
         xs, acc, wq, wo, wi, wd, sem = refs[6:]
@@ -280,12 +304,12 @@
 
     @pl.when(layer == 0)
     def _():
-        start_weights(tab, 0, w_hbm, weights(0), sem.at[0])
+        start_weights(held, tab, 0, w_hbm, weights(0), sem.at[0])
         xs[...] = x_ref[...]
 
     @pl.when(layer + 1 < LAYERS)
     def _():
-        start_weights(tab, layer + 1, w_hbm, weights(nxt), sem.at[nxt])
+        start_weights(held, tab, layer + 1, w_hbm, weights(nxt), sem.at[nxt])
 
     mine, msem = weights(buf), sem.at[buf]
     if keep:
@@ -294,7 +318,8 @@
     else:
         qkv, o_all = qkv_s, o_s
     hat, _ = normed(xs[...])
-    a_low = (hat * vec_ref[0, 0:1, :] + vec_ref[0, 1:2, :]).astype(bf16)
+    row = lambda k: vec_ref[pl.ds(1 + 4 * layer + k, 1), :]
+    a_low = (hat * row(0) + row(1)).astype(bf16)
     wait_weights(w_hbm, mine, msem, range(16))
     m0, m1, first = head_masks()
 
@@ -317,7 +342,7 @@
     if keep:
         h_ref[0] = h
     hat, _ = normed(h)
-    c_low = (hat * vec_ref[0, 2:3, :] + vec_ref[0, 3:4, :]).astype(bf16)
+    c_low = (hat * row(2) + row(3)).astype(bf16)
     acc[...] = jnp.zeros_like(acc)
 
     def mlp(cc, carry):
@@ -347,7 +372,8 @@
             out_ref[...] = out_ref[...] + unit
 
 
-def encoder(tab, x, vecs, slots, keep):
+def encoder(held, tab, x, vecs, slots, keep):
+    table = pl.BlockSpec((VROWS, D), lambda l, tab: (0, 0))
     whole = pl.BlockSpec((F, D), lambda l, tab: (0, 0))
     per = lambda *s: pl.BlockSpec((1,) + s, lambda l, tab: (l,) + (0,) * len(s))
     outs = [jax.ShapeDtypeStruct((F, D), f32)]
@@ -368,12 +394,12 @@
     else:
         scratch += [pltpu.VMEM((6, F, BLK), bf16), pltpu.VMEM((2, F, BLK), bf16)]
     return pl.pallas_call(
-        functools.partial(encoder_kernel, keep),
+        functools.partial(encoder_kernel, keep, held),
         out_shape=outs,
         grid_spec=pltpu.PrefetchScalarGridSpec(
             num_scalar_prefetch=1,
             grid=(LAYERS,),
-            in_specs=[whole, per(8, D), ANY],
+            in_specs=[whole, table, ANY],
             out_specs=out_specs,
             scratch_shapes=scratch,
         ),
@@ -384,12 +410,12 @@
 
 
 def head_kernel(
-    tab, x_ref, vec_ref, target_ref, mask_ref, scale_ref, w_hbm, dx_ref, grad_ref, vg_ref, loss_ref, wh, sem
+    held, tab, starts_ref, x_ref, vec_ref, target_ref, w_hbm, dx_ref, grad_ref, vg_ref, loss_ref, wh, sem
 ):
     copies = []
     for t in range(2):
         for r in range(2):
-            src = tab[t * NBLK + 24 * LAYERS + r]
+            src = spot_of(held, tab, t, 24 * LAYERS + r)
             copies.append(
                 pltpu.make_async_copy(
                     w_hbm.at[src], wh.at[t, pl.ds(r * BLK, BLK), :], sem.at[t * 2 + r]
@@ -397,10 +423,13 @@
             )
             copies[-1].start()
     hat, spread = normed(x_ref[...])
-    gain = vec_ref[0:1, :]
-    low = (hat * gain + vec_ref[1:2, :]).astype(bf16)
-    row_mask = mask_ref[...]
-    scale = scale_ref[0, 0]
+    at = 1 + 4 * LAYERS
+    gain = vec_ref[at : at + 1, :]
+    low = (hat * gain + vec_ref[at + 1 : at + 2, :]).astype(bf16)
+    row_mask = span_row(starts_ref, lax.axis_index("tensor"), 0)
+    counts = COUNT_BASE * vec_ref[COUNT_AT : COUNT_AT + 1, :] + vec_ref[COUNT_AT + 1 : COUNT_AT + 2, :]
+    masked = jnp.sum(counts, axis=1, keepdims=True) / (D // lax.axis_size("dp"))
+    scale = 1.0 / (masked * math.sqrt(D))
     for c in copies:
         c.wait()
     total = jnp.zeros((F, 1), f32)
@@ -423,10 +452,10 @@
     dx_ref[...] = norm_back(grad, hat, spread, gain)
 
 
-def head(tab, x, vec, target, mask_col, scale, slots):
+def head(held, tab, mask_starts, x, vec, target, slots):
     whole = lambda *s: pl.BlockSpec(s, lambda i, tab: (0,) * len(s))
     return pl.pallas_call(
-        head_kernel,
+        functools.partial(head_kernel, held),
         out_shape=[
             jax.ShapeDtypeStruct((F, D), f32),
             jax.ShapeDtypeStruct((4, BLK, BLK), bf16),
@@ -437,24 +466,23 @@
             num_scalar_prefetch=1,
             grid=(1,),
             in_specs=[
+                pl.BlockSpec(memory_space=pltpu.SMEM),
                 whole(F, D),
-                whole(8, D),
+                whole(VROWS, D),
                 whole(F, D),
-                whole(F, 1),
-                pl.BlockSpec(memory_space=pltpu.SMEM),
                 ANY,
             ],
             out_specs=[whole(F, D), whole(4, BLK, BLK), whole(8, D), whole(8, 128)],
             scratch_shapes=[pltpu.VMEM((2, D, BLK), bf16), pltpu.SemaphoreType.DMA((4,))],
         ),
         compiler_params=pltpu.CompilerParams(vmem_limit_bytes=VLIM),
-    )(tab, x, vec, target, mask_col, scale, slots)
+    )(tab, mask_starts, x, vec, target, slots)
 
 
 def back_kernel(
+    held,
     slot_total,
     tab,
-    used,
     dx_ref,
     vec_ref,
     xin_ref,
@@ -480,27 +508,39 @@
     gsem,
     hsem,
     zsem,
+    used,
 ):
     step = pl.program_id(0)
     layer = LAYERS - 1 - step
     mine = [wq, wo, wi, wd]
-    start_weights(tab, layer, w_hbm, mine, sem)
+    start_weights(held, tab, layer, w_hbm, mine, sem)
     plan = weight_plan()
 
     def head_copy(i):
-        dst = tab[(i // 2) * NBLK + 24 * LAYERS + i % 2]
+        dst = spot_of(held, tab, i // 2, 24 * LAYERS + i % 2)
         return pltpu.make_async_copy(head_ref.at[i], grads_hbm.at[dst], hsem.at[i])
 
     half_slots = slot_total // 2
 
     def zero_copy(s, t):
-        at = used[slot_total // 2 + s] + t * used[2 * (slot_total // 2)]
+        at = lax.div(s, held) * (2 * held) + t * held + lax.rem(s, held)
         return pltpu.make_async_copy(zero, grads_hbm.at[at], zsem.at[s, t])
 
     @pl.when(step == 0)
     def _():
         dxs[...] = dx_ref[...]
         zero[...] = jnp.zeros_like(zero)
+
+        def clear(s, carry):
+            used[s] = 0
+            return carry
+
+        def mark(b, carry):
+            used[tab[b]] = 1
+            return carry
+
+        lax.fori_loop(0, half_slots, clear, 0)
+        lax.fori_loop(0, NBLK, mark, 0)
         for i in range(4):
             head_copy(i).start()
 
@@ -518,11 +558,12 @@
         return pltpu.make_async_copy(stage.at[k], grads_hbm.at[dst], gsem.at[k])
 
     def send(k, off, t):
-        grad_copy(k, tab[t * NBLK + layer * 24 + off]).start()
+        grad_copy(k, spot_of(held, tab, t, layer * 24 + off)).start()
 
     low = dxs[...].astype(bf16)
+    row = lambda k: vec_ref[pl.ds(1 + 4 * layer + k, 1), :]
     hat2, spread2 = normed(h_ref[0])
-    c_low = (hat2 * vec_ref[0, 2:3, :] + vec_ref[0, 3:4, :]).astype(bf16)
+    c_low = (hat2 * row(2) + row(3)).astype(bf16)
     acc[...] = jnp.zeros_like(acc)
 
     def mlp(cc, carry):
@@ -545,11 +586,11 @@
     grad = acc[...]
     vg_ref[0, 2:3, :] = jnp.sum(grad * hat2, axis=0, keepdims=True)
     vg_ref[0, 3:4, :] = jnp.sum(grad, axis=0, keepdims=True)
-    grad_h = dxs[...] + norm_back(grad, hat2, spread2, vec_ref[0, 2:3, :])
+    grad_h = dxs[...] + norm_back(grad, hat2, spread2, row(2))
     dxs[...] = grad_h
     low_h = grad_h.astype(bf16)
     hat1, spread1 = normed(xin_ref[0])
-    a_low = (hat1 * vec_ref[0, 0:1, :] + vec_ref[0, 1:2, :]).astype(bf16)
+    a_low = (hat1 * row(0) + row(1)).astype(bf16)
     acc[...] = jnp.zeros_like(acc)
     wait_weights(w_hbm, mine, sem, range(16))
     m0, m1, _ = head_masks()
@@ -589,7 +630,7 @@
     grad = acc[...]
     vg_ref[0, 0:1, :] = jnp.sum(grad * hat1, axis=0, keepdims=True)
     vg_ref[0, 1:2, :] = jnp.sum(grad, axis=0, keepdims=True)
-    grad_x = dxs[...] + norm_back(grad, hat1, spread1, vec_ref[0, 0:1, :])
+    grad_x = dxs[...] + norm_back(grad, hat1, spread1, row(0))
     dxs[...] = grad_x
     out_ref[...] = grad_x
     for k in range(48):
@@ -611,25 +652,25 @@
         lax.fori_loop(0, half_slots, done, 0)
 
 
-def backward(tab, used, grad_x, vecs, saved, head_grad, slots):
+def backward(held, tab, grad_x, vecs, saved, head_grad, slots):
     slot_total = slots.shape[0]
-    whole = lambda *s: pl.BlockSpec(s, lambda i, tab, used: (0,) * len(s))
+    whole = lambda *s: pl.BlockSpec(s, lambda i, tab: (0,) * len(s))
     per = lambda *s: pl.BlockSpec(
-        (1,) + s, lambda i, tab, used: (LAYERS - 1 - i,) + (0,) * len(s)
+        (1,) + s, lambda i, tab: (LAYERS - 1 - i,) + (0,) * len(s)
     )
     return pl.pallas_call(
-        functools.partial(back_kernel, slot_total),
+        functools.partial(back_kernel, held, slot_total),
         out_shape=[
             jax.ShapeDtypeStruct((F, D), f32),
             jax.ShapeDtypeStruct(slots.shape, bf16),
             jax.ShapeDtypeStruct((LAYERS, 8, D), f32),
         ],
         grid_spec=pltpu.PrefetchScalarGridSpec(
-            num_scalar_prefetch=2,
+            num_scalar_prefetch=1,
             grid=(LAYERS,),
             in_specs=[
                 whole(F, D),
-                per(8, D),
+                whole(VROWS, D),
                 per(F, D),
                 per(6, F, BLK),
                 per(2, F, BLK),
@@ -652,18 +693,22 @@
                 pltpu.SemaphoreType.DMA((48,)),
                 pltpu.SemaphoreType.DMA((4,)),
                 pltpu.SemaphoreType.DMA((slot_total // 2, 2)),
+                pltpu.SMEM((slot_total // 2,), jnp.int32),
             ],
         ),
         compiler_params=pltpu.CompilerParams(
             dimension_semantics=("arbitrary",), vmem_limit_bytes=VLIM
         ),
-    )(tab, used, grad_x, vecs, *saved, head_grad, slots)
+    )(tab, grad_x, vecs, *saved, head_grad, slots)
 
 
 MESH = pl.DeviceIdType.MESH
 ZS = 4
-SPLIT = (336, 560, 640)
+SPLIT = (368, 496, 672)
 ORDERS = ("xyz", "zxy", "zyx", "zxy")
+DENSE = 3
+RANK = {3: 0, 1: 1, 2: 2, 0: 3}
+WEIGHT = {0: -1, 1: 0, 2: 0, 3: 2}
 
 
 def place():
@@ -699,25 +744,60 @@
 
 def piece_order():
     pieces = []
-    for cls in (3, 1, 2, 0):
+    for cls in range(len(ORDERS)):
         for dz in range(1 - ZS, ZS):
             for dx in range(2):
                 for dt in range(2):
                     pieces.append((abs(dz) + dx + dt, cls, dz, dx, dt))
-    rank = {3: 0, 1: 1, 2: 2, 0: 3}
-    pieces.sort(key=lambda p: (p[0], rank[p[1]], abs(p[2])))
+    pieces.sort(key=lambda p: (p[0] + WEIGHT[p[1]], RANK[p[1]], abs(p[2])))
     return pieces
 
 
-def gather_kernel(x_ref, d_ref, out_ref, dout_ref, ssem, rsem, csem, crsem, lsem):
+def span_row(starts, clip, axis):
+    shape = (1, F) if axis else (F, 1)
+    at = lax.broadcasted_iota(jnp.int32, shape, axis)
+    inside = jnp.zeros(shape, f32)
+    for span in range(SPANS):
+        begin = starts[clip, span]
+        inside = jnp.where((at >= begin) & (at < begin + MASK_LEN), 1.0, inside)
+    return inside
+
+
+def gather_kernel(starts_ref, full_ref, cols_ref, out_ref, dout_ref, x_ref, d_ref, ssem, rsem, csem, crsem, lsem):
     z, x, c, t = place()
-    starts = (0, SPLIT[0], SPLIT[0] + SPLIT[1])
+    half = d_ref.shape[0]
+    cols = cols_ref[pl.ds(pl.multiple_of(t * half, half), half), :]
+    lane = lax.broadcasted_iota(jnp.int32, (1, 128), 1)
+    cut = (C + CONV) // 128 * 128
+    width = cols.shape[1] - cut
+    tail = jnp.concatenate([cols[:, cut:], jnp.zeros((half, 128 - width), f32)], axis=1)
+    d_ref[:, :cut] = cols[:, :cut].astype(bf16)
+    d_ref[:, cut : cut + 128] = jnp.where(lane < C + CONV - cut, tail, 0.0).astype(bf16)
+    if cut + 128 < VEC_AT:
+        d_ref[:, cut + 128 : VEC_AT] = jnp.zeros((half, VEC_AT - cut - 128), bf16)
+    vec = pltpu.roll(tail, 128 - (C + CONV - cut), 1)
+    count = jnp.zeros((1, 1), f32)
+    for clip in range(starts_ref.shape[0]):
+        count = count + jnp.sum(span_row(starts_ref, clip, 1), axis=1, keepdims=True)
+    high = jnp.floor(count * (1.0 / COUNT_BASE))
+    vec = jnp.where(lane < NVEC, vec, 0.0)
+    vec = jnp.where(lane == COUNT_AT, high, vec)
+    vec = jnp.where(lane == COUNT_AT + 1, count - COUNT_BASE * high, vec)
+    d_ref[:, VEC_AT:] = vec.astype(bf16)
+
+    def cast(k, carry):
+        part = pl.ds(pl.multiple_of(k * 128, 128), 128)
+        x_ref[part, :] = full_ref[part, :].astype(bf16)
+        return carry
+
+    lax.fori_loop(0, x_ref.shape[0] // 128, cast, 0)
+    starts = [sum(SPLIT[:i]) for i in range(len(SPLIT))]
 
     def rows(cls):
         return pl.ds(starts[cls], SPLIT[cls])
 
     def spot(cls, zo, xo, co, to):
-        if cls == 3:
+        if cls == DENSE:
             return dout_ref.at[zo, xo, co, to]
         return out_ref.at[zo, xo, co, to, rows(cls), :]
 
@@ -766,7 +846,7 @@
         valid = None if dz == 0 else ((zo >= 0) & (zo < ZS))
         at = (zo, xo, to)
         if last < 0:
-            if cls == 3:
+            if cls == DENSE:
                 src = d_ref
             else:
                 src = x_ref.at[rows(cls), :]
@@ -811,7 +891,7 @@
             copy.wait_send()
         else:
             pl.when(cond)(copy.wait_send)
-    for cls in range(4):
+    for cls in range(len(ORDERS)):
         for zo in range(ZS):
             for xo in range(2):
                 for to in range(2):
@@ -826,29 +906,38 @@
                     ).wait_recv()
 
 
-def ring_gather(flat_slots, cols):
+def ring_gather(mask_starts, flat_slots, cols):
     rows, width = flat_slots.shape
+    half = cols.shape[0] // 2
+    n = len(ORDERS)
+    vm = pl.BlockSpec(memory_space=pltpu.VMEM)
     return pl.pallas_call(
         gather_kernel,
         out_shape=[
             jax.ShapeDtypeStruct((ZS, 2, 2, 2, rows, width), bf16),
-            jax.ShapeDtypeStruct((ZS, 2, 2, 2) + cols.shape, bf16),
+            jax.ShapeDtypeStruct((ZS, 2, 2, 2, half, WIDE), bf16),
         ],
-        in_specs=[pl.BlockSpec(memory_space=pltpu.VMEM)] * 2,
+        in_specs=[pl.BlockSpec(memory_space=pltpu.SMEM), vm, vm],
         out_specs=[pl.BlockSpec(memory_space=pl.ANY)] * 2,
         scratch_shapes=[
-            pltpu.SemaphoreType.DMA((4, 4, 16)),
-            pltpu.SemaphoreType.DMA((4, 16)),
-            pltpu.SemaphoreType.DMA((4, 16)),
-            pltpu.SemaphoreType.DMA((4, 16)),
+            pltpu.VMEM((rows, width), bf16),
+            pltpu.VMEM((half, WIDE), bf16),
+            pltpu.SemaphoreType.DMA((4, n, 16)),
+            pltpu.SemaphoreType.DMA((n, 16)),
+            pltpu.SemaphoreType.DMA((n, 16)),
+            pltpu.SemaphoreType.DMA((n, 16)),
             pltpu.SemaphoreType.DMA((2,)),
         ],
         compiler_params=pltpu.CompilerParams(collective_id=0, has_side_effects=True),
-    )(flat_slots, cols)
+    )(mask_starts, flat_slots, cols)
+
 
 RING = 4
-PIECE = ((336, 384), (560, 384), (640, 384), (24, 1664))
-CHUNK = (112, 112, 128, 24)
+PIECE = tuple((n, 384) for n in SPLIT) + ((24, WIDE),)
+
+
+def chunk_of(n):
+    return max(k for k in range(8, 137, 8) if n % k == 0)
 
 
 def coord(dim, at):
@@ -872,12 +961,13 @@
 
 
 def scatter_kernel(g_ref, dg_ref, out_ref, dout_ref, acc, dacc, *rest):
-    bufs = [rest[3 * i : 3 * i + 3] for i in range(4)]
-    ring, dring = rest[12:14]
-    csem, crsem, ssem, osem = rest[14:18]
-    rsems = [rest[18 + 3 * i : 21 + 3 * i] for i in range(4)]
+    bufs = [rest[3 * i : 3 * i + 3] for i in range(len(ORDERS))]
+    ring, dring = rest[3 * len(ORDERS) : 3 * len(ORDERS) + 2]
+    csem, crsem, ssem, osem = rest[3 * len(ORDERS) + 2 : 3 * len(ORDERS) + 6]
+    base = 3 * len(ORDERS) + 6
+    rsems = [rest[base + 3 * i : base + 3 + 3 * i] for i in range(len(ORDERS))]
     z, x, c, t = place()
-    starts = (0, SPLIT[0], SPLIT[0] + SPLIT[1])
+    starts = [sum(SPLIT[:i]) for i in range(len(SPLIT))]
 
     def rows(cls):
         return pl.ds(starts[cls], SPLIT[cls])
@@ -886,12 +976,12 @@
         return (at[0] * 2 + at[1]) * 2 + at[2]
 
     def mine(cls, at, co):
-        if cls == 3:
+        if cls == DENSE:
             return dg_ref.at[at[0], at[1], co, at[2]]
         return g_ref.at[at[0], at[1], co, at[2], rows(cls), :]
 
     def held(cls, f):
-        if cls == 3:
+        if cls == DENSE:
             return dacc.at[f]
         return acc.at[f, rows(cls), :]
 
@@ -909,7 +999,7 @@
 
     def own_copy(i):
         cls, _, _, _, at, _ = plan[i]
-        if cls == 3:
+        if cls == DENSE:
             dst = dring.at[i % RING]
         else:
             dst = ring.at[i % RING, pl.ds(0, SPLIT[cls]), :]
@@ -975,7 +1065,7 @@
             core_copies[i].wait_recv()
             for ref, sem in fixed:
                 arrive(ref, sem)
-            size, chunk = PIECE[cls][0], CHUNK[cls]
+            size, chunk = PIECE[cls][0], chunk_of(PIECE[cls][0])
 
             def add_up(extra):
                 refs = [dst, own] + [r for r, _ in fixed] + extra
@@ -986,7 +1076,7 @@
                     for r in refs[1:]:
                         total = total + r[at_rows, :].astype(f32)
                     if last < 0:
-                        if cls == 3:
+                        if cls == DENSE:
                             dout_ref[at_rows, :] = total
                         else:
                             out_ref[pl.ds(starts[cls] + k * chunk, chunk), :] = total
@@ -1066,13 +1156,13 @@
     rows, width = g.shape[-2:]
     scratch = [pltpu.VMEM((16, rows, width), bf16), pltpu.VMEM((16,) + dg.shape[-2:], bf16)]
     sems = []
-    for cls in range(4):
+    for cls in range(len(ORDERS)):
         for dim in "zxy":
             n = free_size(cls, dim) * (ZS + 1 if dim == "z" else 1)
             scratch.append(pltpu.VMEM((n,) + PIECE[cls], bf16))
             sems.append(pltpu.SemaphoreType.DMA((n,)))
-    scratch += [pltpu.VMEM((RING, 640, width), bf16), pltpu.VMEM((RING, 24, 1664), bf16)]
-    scratch += [pltpu.SemaphoreType.DMA((4, 16))] * 3 + [pltpu.SemaphoreType.DMA((RING,))]
+    scratch += [pltpu.VMEM((RING, max(SPLIT), width), bf16), pltpu.VMEM((RING, 24, WIDE), bf16)]
+    scratch += [pltpu.SemaphoreType.DMA((len(ORDERS), 16))] * 3 + [pltpu.SemaphoreType.DMA((RING,))]
     return pl.pallas_call(
         scatter_kernel,
         out_shape=[
@@ -1174,16 +1264,104 @@
     )(red, dred, loss_tile)
 
 
-def span_mask(mask_starts, frames):
-    positions = jnp.arange(frames, dtype=jnp.int32)[None, :, None]
+def update_kernel(
+    set_ref, tile_ref, grad_ref, mat_ref, mom_ref, stat_ref, root_ref, teach_ref, *refs
+):
+    cols_ref, dense_ref, dm_ref, ds_ref, td_ref = refs[:5]
+    mat_new, mom_new, stat_new, teach_new, dense_new, dm_new, ds_new, td_new, norm_new = refs[5:]
+    norm = jnp.sqrt(tile_ref[1:2, 0:1])
+    rate = set_ref[0]
+    factor = jnp.minimum(1.0, set_ref[1] / norm)
+    half = 1.0 - state_decay
+    grad = grad_ref[0]
+    low = grad.astype(bf16)
+    weight = half * factor * factor
+    stat_new[0, 0, 0] = state_decay * stat_ref[0, 0, 0] + weight * nt(low, low)
+    stat_new[0, 0, 1] = state_decay * stat_ref[0, 0, 1] + weight * tn(low, low)
+
+    def split(v):
+        high = v.astype(bf16)
+        return high, (v - high.astype(f32)).astype(bf16)
+
+    left_high, left_low = split(root_ref[0, 0, 0])
+    right_high, right_low = split(root_ref[0, 0, 1])
+    side_high, side_low = split(nn(left_high, low) + nn(left_low, low))
+    precond = nn(side_high, right_high) + nn(side_low, right_high) + nn(side_high, right_low)
+    momentum = state_decay * mom_ref[0, 0] + (half * factor) * precond
+    mom_new[0, 0] = momentum
+    matrix = mat_ref[0, 0] - matrix_rate * momentum
+    mat_new[0, 0] = matrix
+    teach_new[0, 0] = rate * teach_ref[0, 0] + (1.0 - rate) * matrix
+
+    @pl.when(pl.program_id(0) == 0)
+    def _():
+        norm_new[...] = jnp.broadcast_to(norm, (8, 128))
+        cut = (C + CONV) // 128 * 128
+        tail = dense_ref.shape[1] - cut
+        lane = lax.broadcasted_iota(jnp.int32, (1, 128), 1)
+        shift = C + CONV - cut
+        vec = pltpu.roll(cols_ref[:, VEC_AT : VEC_AT + 128], shift, 1)
+        last = jnp.where(lane < shift, cols_ref[:, cut : cut + 128], vec)
+        for at, size, raw in ((0, cut, cols_ref[:, :cut]), (cut, tail, last[:, :tail])):
+            part = slice(at, at + size)
+            small = raw * factor
+            first = state_decay * dm_ref[:, part] + half * small
+            second = state_decay * ds_ref[:, part] + half * small * small
+            dm_new[:, part] = first
+            ds_new[:, part] = second
+            new = dense_ref[:, part] - dense_rate * first / (jnp.sqrt(second) + adam_eps)
+            dense_new[:, part] = new
+            td_new[:, part] = rate * td_ref[:, part] + (1.0 - rate) * new
+
+
+def update(settings, tile, grads, blocks, cols, dense):
+    matrices, momentum, statistics, inverse_roots, teacher = blocks
+    held = matrices.shape[0]
+    one = pl.BlockSpec((1, 1, BLK, BLK), lambda i: (i, 0, 0, 0))
+    two = pl.BlockSpec((1, 1, 2, BLK, BLK), lambda i: (i, 0, 0, 0, 0))
+    whole = lambda v: pl.BlockSpec(v.shape, lambda i: (0,) * v.ndim)
+    like = lambda v: jax.ShapeDtypeStruct(v.shape, f32)
+    tile_spec = pl.BlockSpec((8, 128), lambda i: (0, 0))
+    return pl.pallas_call(
+        update_kernel,
+        grid=(held,),
+        out_shape=[like(matrices), like(momentum), like(statistics), like(teacher)]
+        + [like(v) for v in dense]
+        + [jax.ShapeDtypeStruct((8, 128), f32)],
+        in_specs=[
+            pl.BlockSpec(memory_space=pltpu.SMEM),
+            tile_spec,
+            pl.BlockSpec((1, BLK, BLK), lambda i: (i, 0, 0)),
+            one,
+            one,
+            two,
+            two,
+            one,
+            whole(cols),
+        ]
+        + [whole(v) for v in dense],
+        out_specs=[one, one, two, one] + [whole(v) for v in dense] + [tile_spec],
+        compiler_params=pltpu.CompilerParams(vmem_limit_bytes=VLIM),
+    )(settings, tile, grads, matrices, momentum, statistics, inverse_roots, teacher, cols, *dense)
+
+
+def ringed():
+    return lax.axis_size("dp") == 4 * ZS and lax.axis_size("tensor") == 2
+
+
+def span_count(mask_starts):
+    positions = jnp.arange(F, dtype=jnp.int32)[None, :, None]
     starts = mask_starts[:, None, :]
     inside = (positions >= starts) & (positions < starts + MASK_LEN)
-    return jnp.any(inside, axis=-1).astype(f32)
-
-
-def widen(cols, digits):
+    return jnp.sum(jnp.any(inside, axis=-1).astype(f32))
+
+
+def widen(cols, mask_starts):
     rows = cols.shape[0]
     end = C + CONV
+    count = span_count(mask_starts)
+    high = jnp.floor(count / COUNT_BASE)
+    digits = jnp.stack([high, count - COUNT_BASE * high])
     return jnp.concatenate(
         [
             cols[:, :end],
@@ -1197,32 +1375,14 @@
     )
 
 
-def narrow(cols):
-    return jnp.concatenate([cols[:, : C + CONV], cols[:, VEC_AT : VEC_AT + NVEC]], axis=1)
-
-
-def vectors_of(dense_low):
-    rows = dense_low[:, VEC_AT : VEC_AT + 16].T.astype(f32)
-    per_layer = rows[1 : 1 + 4 * LAYERS].reshape(LAYERS, 4, D)
-    per_layer = jnp.pad(per_layer, ((0, 0), (0, 4), (0, 0)))
-    final = jnp.pad(rows[1 + 4 * LAYERS : 3 + 4 * LAYERS], ((0, 6), (0, 0)))
-    return per_layer, final
-
-
-def gather_params(local_slots, cols, digits):
-    low = local_slots[:, 0].astype(bf16)
-    wide = widen(cols.astype(bf16), digits)
+def gather_params(mask_starts, local_slots, cols):
     if not ringed():
+        low = local_slots[:, 0].astype(bf16)
+        wide = widen(cols, mask_starts).astype(bf16)
         slots = lax.all_gather(low, ("dp", "tensor"), axis=0, tiled=True)
         return slots, lax.all_gather(wide, "dp", axis=0, tiled=True)
-    half = wide.shape[0] // 2
-    part = lax.dynamic_slice_in_dim(wide, lax.axis_index("tensor") * half, half, axis=0)
-    slots, dense = ring_gather(low.reshape(-1, BLK), part)
+    slots, dense = ring_gather(mask_starts, local_slots.reshape(-1, BLK), cols)
     return slots.reshape(-1, BLK, BLK), dense.reshape(-1, WIDE)
-
-
-def ringed():
-    return lax.axis_size("dp") == 4 * ZS and lax.axis_size("tensor") == 2
 
 
 def reduce_grads(slot_part, col_part, loss_tile):
@@ -1233,12 +1393,14 @@
         reduced = slot_sum.astype(f32)
         square = jnp.sum(reduced * reduced) + 0.5 * jnp.sum(col_sum * col_sum)
         loss_value, square_sum = lax.psum((loss_tile[0, 0], square), ("dp", "tensor"))
-        return reduced, col_sum, loss_value, square_sum
+        row = jnp.arange(8)[:, None]
+        tile = jnp.where(row == 0, loss_value, jnp.broadcast_to(square_sum, (8, 128)))
+        return reduced, col_sum, tile
     shape = (ZS, 2, 2, 2)
     slots = slot_part.reshape(shape + (-1, BLK))
     slot_sum, col_sum = ring_scatter(slots, col_part.reshape(shape + (-1, WIDE)))
     tile, cols = ring_finish(slot_sum, col_sum, loss_tile)
-    return slot_sum.reshape(-1, BLK, BLK), cols, tile[0, 0], tile[1, 0]
+    return slot_sum.reshape(-1, BLK, BLK), cols, tile
 
 
 def local(
@@ -1257,95 +1419,25 @@
     teacher_dense,
 ):
     held = matrices.shape[0]
-    dp = lax.axis_size("dp")
-    slot_total = held * dp
-    half = lax.axis_index("tensor")
-    masked_all = span_mask(mask_starts, F)
-    count = jnp.sum(masked_all)
-    high = jnp.floor(count / COUNT_BASE)
-    digits = jnp.stack([high, count - COUNT_BASE * high])
-    feat = lax.dynamic_index_in_dim(features, half, axis=0, keepdims=False)
-    masked = lax.dynamic_index_in_dim(masked_all, half, axis=0, keepdims=False)
-    mask_row, mask_col = masked[None, :], masked[:, None]
-
-    base = (block_slot // held) * (2 * held) + block_slot % held
-    tab = jnp.concatenate([base, base + held]).astype(jnp.int32)
-    ids = jnp.arange(slot_total, dtype=jnp.int32)
-    taken = jnp.any(block_slot[None, :] == ids[:, None], axis=1).astype(jnp.int32)
-    places = (ids // held) * (2 * held) + ids % held
-    used = jnp.concatenate([taken, places, jnp.full((8,), held, jnp.int32)]).astype(jnp.int32)
-
-    teach_slots, teach_dense = gather_params(teacher, teacher_dense, digits)
-    low_slots, low_dense = gather_params(matrices, dense_params, digits)
-    counts = low_dense[:: dense_params.shape[0], VEC_AT + COUNT_AT : VEC_AT + COUNT_AT + 2]
-    mask_total = jnp.sum(counts.astype(f32) * jnp.array([COUNT_BASE, 1.0], f32))
-    loss_scale = 1.0 / (mask_total * math.sqrt(D))
-
-    teach_vecs, _ = vectors_of(teach_dense)
-    teach_x = front(teach_dense, feat, mask_row, False)
-    (target,) = encoder(tab, teach_x, teach_vecs, teach_slots, False)
-
-    vecs, final_vec = vectors_of(low_dense)
-    x0, emb, conv_out = front(low_dense, feat, mask_row, True)
-    x_last, *saved = encoder(tab, x0, vecs, low_slots, True)
+    teach_slots, teach_dense = gather_params(mask_starts, teacher, teacher_dense)
+    teach_x, teach_vecs = front(mask_starts, teach_dense, features, False)
+    (target,) = encoder(held, block_slot, teach_x, teach_vecs, teach_slots, False)
+
+    slots, dense = gather_params(mask_starts, matrices, dense_params)
+    x0, vecs, emb, conv_out = front(mask_starts, dense, features, True)
+    x_last, *saved = encoder(held, block_slot, x0, vecs, slots, True)
     grad_x, head_grad, head_vg, loss_tile = head(
-        tab, x_last, final_vec, target, mask_col, loss_scale.reshape(1, 1), low_slots
+        held, block_slot, mask_starts, x_last, vecs, target, slots
     )
-    grad_x, slot_part, layer_vg = backward(
-        tab, used, grad_x, vecs, saved, head_grad, low_slots
+    grad_x, slot_part, layer_vg = backward(held, block_slot, grad_x, vecs, saved, head_grad, slots)
+    col_part = front_back(mask_starts, dense, features, grad_x, emb, conv_out, layer_vg, head_vg)
+    reduced, cols, tile = reduce_grads(slot_part, col_part, loss_tile)
+    blocks = (matrices, momentum, statistics, inverse_roots, teacher)
+    dense_state = (dense_params, dense_moment, dense_second, teacher_dense)
+    mat, mom, stat, teach, dense_new, dm_new, ds_new, td_new, norm = update(
+        settings, tile, reduced, blocks, cols, dense_state
     )
-    vec_rows = jnp.concatenate(
-        [
-            jnp.zeros((1, D), f32),
-            layer_vg[:, :4].reshape(4 * LAYERS, D),
-            head_vg[:2],
-            jnp.zeros((128 - NVEC, D), f32),
-        ],
-        axis=0,
-    )
-    col_part = front_back(low_dense, feat, mask_row, grad_x, emb, conv_out, vec_rows)
-
-    reduced, cols, loss_value, square_sum = reduce_grads(slot_part, col_part, loss_tile)
-    reduced_cols = narrow(cols)
-    grad_norm = jnp.sqrt(square_sum)
-    factor = jnp.minimum(1.0, settings[1] / grad_norm)
-    squared = factor * factor
-    low = reduced.astype(bf16)
-    left_new = state_decay * statistics[:, 0, 0] + ((1.0 - state_decay) * squared) * jnp.einsum(
-        "sij,skj->sik", low, low, preferred_element_type=f32
-    )
-    right_new = state_decay * statistics[:, 0, 1] + ((1.0 - state_decay) * squared) * jnp.einsum(
-        "sji,sjk->sik", low, low, preferred_element_type=f32
-    )
-    left_side = jnp.einsum(
-        "sij,sjk->sik", inverse_roots[:, 0, 0], reduced, precision=lax.Precision.HIGH
-    )
-    precond = jnp.einsum(
-        "sij,sjk->sik", left_side, inverse_roots[:, 0, 1], precision=lax.Precision.HIGH
-    )
-    momentum_new = state_decay * momentum[:, 0] + ((1.0 - state_decay) * factor) * precond
-    matrices_new = matrices[:, 0] - matrix_rate * momentum_new
-    teacher_new = settings[0] * teacher[:, 0] + (1.0 - settings[0]) * matrices_new
-    statistics_new = jnp.stack([left_new, right_new], axis=1)[:, None]
-    grad_small = reduced_cols * factor
-    dense_moment_new = state_decay * dense_moment + (1.0 - state_decay) * grad_small
-    dense_second_new = state_decay * dense_second + (1.0 - state_decay) * grad_small * grad_small
-    dense_new = dense_params - dense_rate * dense_moment_new / (
-        jnp.sqrt(dense_second_new) + adam_eps
-    )
-    teacher_dense_new = settings[0] * teacher_dense + (1.0 - settings[0]) * dense_new
-    return (
-        loss_value,
-        grad_norm,
-        matrices_new[:, None],
-        momentum_new[:, None],
-        statistics_new,
-        teacher_new[:, None],
-        dense_new,
-        dense_moment_new,
-        dense_second_new,
-        teacher_dense_new,
-    )
+    return tile[0, 0], norm[0, 0], mat, mom, stat, teach, dense_new, dm_new, ds_new, td_new
 
 
 def solution(mesh):

time: 724 us -> 669 us (0.924)
  other arithmetic: 20.1 us -> 0 us
  local copies, waits for them, and re-layouts: 18.2 us -> 2.36 us
  matrix products: 10.4 us -> 0 us
    pallas_call x4 -> x5, Pallas kernels: 119 us -> 134 us  [the longest x1 58.1 us: backward(): pl.pallas_call(functools.partial(back_kernel, held, slot_total), out_shap...]
    pallas_call x1, Pallas kernels: 26.8 us -> 16.1 us  [ring_finish(): pl.pallas_call(finish_kernel, out_shape=[jax.ShapeDtypeStruct((8, 128), f...]
    dot_general x4 -> x0, matrix products: 10.4 us -> none  [the longest x1 4.25 us: local(): jnp.einsum('sij,sjk->sik', left_side, inverse_roots[:, 0, 1], precision=l...]
    pallas_call x2, Pallas kernels: 328 us -> 318 us  [ring_gather(): pl.pallas_call(gather_kernel, out_shape=[jax.ShapeDtypeStruct((ZS, 2, 2,...]
where the time goes in v2:
time: 669 us; the launch traced here: 662 us
  Pallas kernels  658 us (98%)
    pallas_call x2, Pallas kernels, ring_gather(): pl.pallas_call(gather_kernel, out_shape=[jax.ShapeDtypeStruct((ZS, 2, 2,...  318 us
    pallas_call x1, Pallas kernels, ring_scatter(): pl.pallas_call(scatter_kernel, out_shape=[jax.ShapeDtypeStruct((rows, wid...  156 us
    pallas_call x1, Pallas kernels, backward(): pl.pallas_call(functools.partial(back_kernel, held, slot_total), out_shap...  58.1 us
    pallas_call x2, Pallas kernels, encoder(): pl.pallas_call(functools.partial(encoder_kernel, keep, held), out_shape=o...  54.7 us
    pallas_call x2, Pallas kernels, front(): pl.pallas_call(functools.partial(front_kernel, keep), out_shape=outs, in_...  17.6 us
    pallas_call x1, Pallas kernels, front_back(): pl.pallas_call(front_back_kernel, out_shape=jax.ShapeDtypeStruct((D, WIDE...  16.3 us
    pallas_call x1, Pallas kernels, ring_finish(): pl.pallas_call(finish_kernel, out_shape=[jax.ShapeDtypeStruct((8, 128), f...  16.1 us
    pallas_call x1, Pallas kernels, update(): pl.pallas_call(update_kernel, grid=(held,), out_shape=[like(matrices), li...  15.1 us

profile of v2, /device:TPU:0, one launch (start us, length us, event | category | flops | bytes accessed | tf_op | source)
XLA Modules:
  0.0 661.8 jit_solution(3935488433323134518)
XLA Ops:
  0.6 160.6 %shard_map.207 = (bf16[4,2,2,2,1536,384]{5,4,3,2,1,0:T(8,128)(2,1)}, bf16[4,2,2,2,24,1664]{5,4,3,2,1,0:T(8,128)(2,1)}) custom-call(s32[2,16]{1,0:T(2,128)} %starts_ref.11, f32[1536,384]{1,0:T(8,128)} %bitcast.20, f32[48,1435]{1,0:T(8,128)} %refs_4_.1), custom_call_target="tpu_custom_call" | custom-call | tf_op jit(solution)/shard_map/pallas_call | solution.py:914
  161.3 8.8 %shard_map.208 = (f32[256,768]{1,0:T(8,128)}, f32[24,768]{1,0:T(8,128)}) custom-call(s32[2,16]{1,0:T(2,128)} %starts_ref.11, bf16[768,1664]{1,0:T(8,128)(2,1)} %bitcast.22, bf16[2,256,512]{2,1,0:T(8,128)(2,1)} %feat_ref.5), custom_call_target="tpu_custom_call" | custom-call | tf_op jit(solution)/shard_map/pallas_call | solution.py:144
  170.0 26.4 %shard_map.209.target_ref = f32[256,768]{1,0:T(8,128)} custom-call(s32[50]{0:T(128)} %tab.7, f32[256,768]{1,0:T(8,128)} %get-tuple-element.52.x_ref, f32[24,768]{1,0:T(8,128)} %get-tuple-element.53.vec_ref, bf16[128,384,384]{2,1,0:T(8,128)(2,1)} %bitcast.15), custom_call_target="tpu_custom_call" | custom-call | tf_op jit(solution)/shard_map/pallas_call | solution.py:396
  196.5 157.8 %shard_map.204 = (bf16[4,2,2,2,1536,384]{5,4,3,2,1,0:T(8,128)(2,1)}, bf16[4,2,2,2,24,1664]{5,4,3,2,1,0:T(8,128)(2,1)}) custom-call(s32[2,16]{1,0:T(2,128)} %starts_ref.11, f32[1536,384]{1,0:T(8,128)} %bitcast.19, f32[48,1435]{1,0:T(8,128)} %refs_1_.1), custom_call_target="tpu_custom_call" | custom-call | tf_op jit(solution)/shard_map/pallas_call | solution.py:914
  354.3 8.8 %shard_map.205 = (f32[256,768]{1,0:T(8,128)}, f32[24,768]{1,0:T(8,128)}, f32[768,256]{1,0:T(8,128)}, f32[768,256]{1,0:T(8,128)}) custom-call(s32[2,16]{1,0:T(2,128)} %starts_ref.11, bf16[768,1664]{1,0:T(8,128)(2,1)} %bitcast.17, bf16[2,256,512]{2,1,0:T(8,128)(2,1)} %feat_ref.5), custom_call_target="tpu_custom_call" | custom-call | tf_op jit(solution)/shard_map/pallas_call | solution.py:144
  363.1 28.2 %shard_map.206 = (f32[256,768]{1,0:T(8,128)}, f32[2,256,768]{2,1,0:T(8,128)}, bf16[2,6,256,384]{3,2,1,0:T(8,128)(2,1)}, bf16[2,2,256,384]{3,2,1,0:T(8,128)(2,1)}...) custom-call(s32[50]{0:T(128)} %tab.7, f32[256,768]{1,0:T(8,128)} %get-tuple-element.47.x_ref, ...), custom_call_target="tpu_custom_call" | custom-call | tf_op jit(solution)/shard_map/pallas_call | solution.py:396
  391.3 6.2 shard_map.210
  397.5 58.1 %shard_map.211 = (f32[256,768]{1,0:T(8,128)}, bf16[128,384,384]{2,1,0:T(8,128)(2,1)}, f32[2,8,768]{2,1,0:T(8,128)}) custom-call(s32[50]{0:T(128)} %tab.7, f32[256,768]{1,0:T(8,128)} %get-tuple-element.55.dx_ref, f32[24,768]{1,0:T(8,128)} %get-tuple-element.48.vec_ref, f32[2,256,768]{2,1,0:T(8,128)} %get-tuple-element.56.xin_ref, ...), custom_call_target="tpu_custom_call" | custom-call | tf_op jit(solution)/shard_map/pallas_call | solution.py:661
  455.6 16.3 %shard_map.212 = bf16[768,1664]{1,0:T(8,128)(2,1)} custom-call(s32[2,16]{1,0:T(2,128)} %starts_ref.11, bf16[768,1664]{1,0:T(8,128)(2,1)} %bitcast.18, bf16[2,256,512]{2,1,0:T(8,128)(2,1)} %feat_ref.5, f32[256,768]{1,0:T(8,128)} %get-tuple-element.63.dx_ref, f32[768,256]{1,0:T(8,128)} %get-tuple-element.64.emb_ref, f32[768,256]{1,0:T(8,128)} %get-tuple-element.65.conv_ref, ...), custom_call_target="tpu_custom_call" | custom-call | tf_op jit(solution)/shard_map/pallas_call | solution.py:214
  472.0 155.7 %shard_map.213 = (f32[1536,384]{1,0:T(8,128)}, f32[24,1664]{1,0:T(8,128)}) custom-call(bf16[4,2,2,2,1536,384]{5,4,3,2,1,0:T(8,128)(2,1)} %bitcast.14, bf16[4,2,2,2,24,1664]{5,4,3,2,1,0:T(8,128)(2,1)} %bitcast.16), custom_call_target="tpu_custom_call" | custom-call | tf_op jit(solution)/shard_map/pallas_call | solution.py:1166
  627.7 16.1 %shard_map.214 = (f32[8,128]{1,0:T(8,128)}, f32[48,1664]{1,0:T(8,128)}) custom-call(f32[1536,384]{1,0:T(8,128)} %get-tuple-element.68.red_ref, f32[24,1664]{1,0:T(8,128)} %get-tuple-element.69.dred_ref, f32[8,128]{1,0:T(8,128)} %get-tuple-element.70.loss_ref), custom_call_target="tpu_custom_call" | custom-call | tf_op jit(solution)/shard_map/pallas_call | solution.py:1247
  643.8 1.2 slice.6
  645.0 15.1 %shard_map.215 = (f32[4,1,384,384]{3,2,1,0:T(8,128)}, f32[4,1,384,384]{3,2,1,0:T(8,128)}, f32[4,1,2,384,384]{4,3,2,1,0:T(8,128)}, f32[4,1,384,384]{3,2,1,0:T(8,1...) custom-call(f32[2]{0:T(128)} %set_ref.1, ...), custom_call_target="tpu_custom_call" | custom-call | tf_op jit(solution)/shard_map/pallas_call | solution.py:1325
  660.2 1.2 slice.7
